TPU v7x, 32 devices: a whole 2x2x4 slice. The times are simulated.
32 devices in a mesh: struct: 8 (over z, x), atom: 4 (over y, core).
Axes of the slice: x: 2, y: 2, z: 4, core: 2. Of those that a mesh axis runs over, the one named last changes fastest.
Arguments:
- atoms_in: bfloat16 [32, 1536, 128], P('struct', 'atom'), parts along dimension 0, may hold values from -6 to 6
- cond: bfloat16 [12288, 128], P(('struct', 'atom')), parts along dimension 0, may hold values from -6 to 6
- pair: bfloat16 [384, 32, 16, 128], P(('struct', 'atom')), parts along dimension 0, may hold values from -6 to 6
- atom_mask: int32 [12288], P(('struct', 'atom')), parts along dimension 0, may hold values 0 or 1
- atom_count: int32 [8], P('struct'), parts along dimension 0, may hold values from 1344 to 1536
- atom_to_token: int32 [12288], P(('struct', 'atom')), parts along dimension 0, may hold values from 0 to 191, as said below
- ada_weight: bfloat16 [2, 128, 256], replicated, may hold values from -0.5 to 0.5
- ada_bias: float32 [2, 128], replicated, may hold values from -1.5 to 1.5
- zero_weight: bfloat16 [2, 128, 128], replicated, may hold values from -0.5 to 0.5
- zero_bias: float32 [2, 128], replicated, may hold values from -2 to 2
- qkvg_weight: bfloat16 [128, 512], replicated, may hold values from -0.5 to 0.5
- query_bias: float32 [128], replicated, may hold values from -4 to 4
- pair_weight: float32 [4, 16], replicated, may hold values from -60 to 60
- out_weight: bfloat16 [128, 128], replicated, may hold values from -0.5 to 0.5
- swiglu_weight: bfloat16 [128, 512], replicated, may hold values from -0.5 to 0.5
- down_weight: bfloat16 [256, 128], replicated, may hold values from -0.375 to 0.375
- token_weight: bfloat16 [128, 768], replicated, may hold values from -0.5 to 0.5
Outputs:
- atoms_out: bfloat16 [32, 1536, 128], P('struct', 'atom'), parts along dimension 0
- tokens_out: bfloat16 [32, 192, 768], P('struct', 'atom'), parts along dimension 0
There are 8 independent parts, one for each index of `struct`. A program takes and returns all parts, laid end to end along the dimension named above; an argument that names none is the same for every part. Nothing has to cross between parts.
Inputs may be any that keep to these rules, and one draw needn't show every extreme that they name: `atom_to_token`: never falls, rises by at most 1 from atom to atom, starts at 0 and ends at 191; an atom a of token t satisfies 8 * t - 8 < a < 8 * t + 2 * 8 - 1.
All inputs are finite; a program needn't handle non-finite values. No bound on the sum of `atom_mask` on one device may be relied on, other than what follows from the above.
Results may differ from a plain program's by a relative error of at most 0.01.
Values may be sent and summed in bfloat16 or wider, within the bound.
A program may use at most 64 MiB of HBM per device.

v0:
```python
import functools

import jax
import jax.numpy as jnp
from jax import lax
from jax.experimental import pallas as pl
from jax.experimental.pallas import tpu as pltpu
from jax.sharding import PartitionSpec as P

ATOMS_PER_TOKEN = 8
EPS = 1e-05
STEPS = 1
DEAD = -1000000000.0
MESH = pl.DeviceIdType.MESH
F32 = jnp.float32
BF16 = jnp.bfloat16


def iota(shape, axis):
    return lax.broadcasted_iota(jnp.int32, shape, axis)


def mm(a, b):
    return jnp.dot(a, b, preferred_element_type=F32)


def two_pieces(values):
    high = values.astype(BF16)
    low = (values - high.astype(F32)).astype(BF16)
    return high, low


def block_body(
    n,
    atoms_hbm, cond_hbm, pair_ref, mask_hbm, token_hbm, count_ref,
    ada_hbm, ada_bias_hbm, zero_hbm, zero_bias_hbm, qkvg_hbm, query_bias_hbm,
    pair_weight_hbm, out_hbm, swiglu_hbm, down_hbm, token_weight_hbm,
    atoms_out_ref, tokens_out_ref,
    atoms_ref, cond_ref, ada_ref, ada_bias_ref, zero_ref, zero_bias_ref, qkvg_ref,
    query_bias_ref, pair_weight_ref, out_ref, swiglu_ref, down_ref, token_weight_ref,
    mask_ref, token_ref,
    pair_buf, halo_x, halo_c, halo_m0, halo_m1, halo_t0, halo_t1, kv_ref, q_ref, gate_ref, bias_ref,
    live_ref, mod_ref, feat_ref, center_ref, mean_ref, lhs_ref, fold_ref,
    edge_out, edge_in, onehot_ref, counts_ref,
    load_sem, pair_sem, send_sem, recv_sem, edge_send_sem, edge_recv_sem,
):
    samples, atoms, width = atoms_ref.shape
    windows, rows_pair, key_len = pair_ref.shape
    heads, channels = pair_weight_ref.shape
    head_dim = width // heads
    query_len = rows_pair // channels
    half = query_len // 2
    margin = (key_len - query_len) // 2
    tokens = tokens_out_ref.shape[1]
    hidden = down_ref.shape[0]
    token_width = token_weight_ref.shape[1]
    rows_half = half * channels

    halo_m, halo_t = (halo_m0, halo_m1), (halo_t0, halo_t1)
    me = lax.axis_index("atom")
    right, left = lax.rem(me + 1, n), lax.rem(me + n - 1, n)

    barrier = pltpu.get_barrier_semaphore()
    for neighbour in (left, right):
        pl.semaphore_signal(barrier, inc=1, device_id={"atom": neighbour}, device_id_type=MESH)

    early = (
        (cond_hbm, cond_ref), (atoms_hbm, atoms_ref), (ada_hbm, ada_ref),
        (ada_bias_hbm, ada_bias_ref), (zero_hbm, zero_ref), (zero_bias_hbm, zero_bias_ref),
        (qkvg_hbm, qkvg_ref), (query_bias_hbm, query_bias_ref),
        (pair_weight_hbm, pair_weight_ref),
    )
    late = (
        (out_hbm, out_ref), (swiglu_hbm, swiglu_ref), (down_hbm, down_ref),
        (token_weight_hbm, token_weight_ref), (mask_hbm, mask_ref), (token_hbm, token_ref),
    )
    loads = [
        pltpu.make_async_copy(src, dst, load_sem.at[i])
        for i, (src, dst) in enumerate(early + late)
    ]
    for copy in loads[: len(early)]:
        copy.start()
    groups = pair_sem.shape[0]
    per_group = windows // groups
    pair_copies = []
    for g in range(groups):
        part = pl.ds(g * per_group, per_group)
        copy = pltpu.make_async_copy(pair_ref.at[part], pair_buf.at[part], pair_sem.at[g])
        copy.start()
        pair_copies.append(copy)
    for copy in loads[len(early) :]:
        copy.start()

    row, col = iota((width, width), 0), iota((width, width), 1)
    inverse = 1.0 / width
    center_ref[...] = (jnp.where(row == col, 1.0, 0.0) - inverse).astype(BF16)
    mean_ref[...] = jnp.full(mean_ref.shape, inverse, F32).astype(BF16)
    kv_ref[:, :, 2 * width :] = jnp.ones((samples, atoms + 2 * margin, width), BF16)
    row, col = iota((rows_half, rows_half), 0), iota((rows_half, rows_half), 1)
    same = jnp.where(row // channels == col // channels, 1.0 / channels, 0.0)
    lhs_ref[pl.ds(0, rows_half)] = (jnp.where(row == col, 1.0, 0.0) - same).astype(BF16)
    folded = rows_half // 2
    fold_ref[...] = jnp.where(
        (iota((half, 2 * folded), 1) % folded) // (channels // 2) == iota((half, 2 * folded), 0),
        1.0 / channels,
        0.0,
    ).astype(BF16)

    pl.semaphore_wait(barrier, 2)

    copies = []
    for side, (target, start) in enumerate(((right, atoms - margin), (left, 0))):
        own = pl.ds(start, margin)
        for which, (src, dst) in enumerate(
            (
                (atoms_hbm.at[:, own], halo_x.at[side]),
                (cond_hbm.at[own], halo_c.at[side]),
                (mask_hbm, halo_m[side]),
                (token_hbm, halo_t[side]),
            )
        ):
            copy = pltpu.make_async_remote_copy(
                src_ref=src,
                dst_ref=dst,
                send_sem=send_sem.at[side, which],
                recv_sem=recv_sem.at[side, which],
                device_id={"atom": target},
                device_id_type=MESH,
            )
            copy.start()
            copies.append(copy)

    for copy in loads[: len(early)]:
        copy.wait()

    def norm(values):
        centred = mm(values, center_ref[...])
        high, low = two_pieces(centred * centred)
        spread = mm(jnp.concatenate([high, low], axis=1), mean_ref[...])
        return centred * lax.rsqrt(spread + EPS)

    cond_norm = norm(cond_ref[...]).astype(BF16)
    for which in range(2):
        adapt = mm(cond_norm, ada_ref[which])
        mod_ref[3 * which] = jax.nn.sigmoid(
            adapt[:, :width] + ada_bias_ref[which : which + 1]
        )
        mod_ref[3 * which + 1] = adapt[:, width:]
        mod_ref[3 * which + 2] = jax.nn.sigmoid(
            mm(cond_norm, zero_ref[which]) + zero_bias_ref[which : which + 1]
        )

    factor = head_dim**-0.5
    for s in range(samples):
        attn_in = (norm(atoms_ref[s]) * mod_ref[0] + mod_ref[1]).astype(BF16)
        projected = mm(attn_in, qkvg_ref[...])
        q_ref[s] = ((projected[:, :width] + query_bias_ref[...]) * factor).astype(BF16)
        kv_ref[s, pl.ds(margin, atoms), pl.ds(0, 2 * width)] = projected[
            :, width : 3 * width
        ].astype(BF16)
        gate_ref[s] = jax.nn.sigmoid(projected[:, 3 * width :])

    weight = pair_weight_ref[...]
    weight = weight - jnp.mean(weight, axis=1, keepdims=True)
    spread_c = jnp.where(
        iota((channels, rows_half), 1) % channels == iota((channels, rows_half), 0), 1.0, 0.0
    ).astype(BF16)
    own_query = iota((half, rows_half), 1) // channels == iota((half, rows_half), 0)
    remaining = weight
    lines = heads * half
    for piece in range(3):
        part = remaining.astype(BF16)
        remaining = remaining - part.astype(F32)
        wide = mm(part, spread_c)
        blocks = [
            jnp.where(own_query, jnp.broadcast_to(wide[h : h + 1], (half, rows_half)), 0.0)
            for h in range(heads)
        ]
        lhs_ref[pl.ds(rows_half + piece * lines, lines)] = jnp.concatenate(
            blocks, axis=0
        ).astype(BF16)
    def pair_window(w):
        block = pair_buf[w]
        both = jnp.concatenate([block[:rows_half], block[rows_half:]], axis=1)
        result = mm(lhs_ref[...], both)
        centred = result[:rows_half]
        at = rows_half
        total = (
            result[at : at + lines]
            + result[at + lines : at + 2 * lines]
            + result[at + 2 * lines : at + 3 * lines]
        )
        square = (centred * centred).reshape(half, 2, channels // 2, 2 * key_len)
        square = (square[:, 0] + square[:, 1]).reshape(folded, 2 * key_len)
        high, low = two_pieces(square)
        spread = mm(fold_ref[...], jnp.concatenate([high, low], axis=0))
        scale = lax.rsqrt(spread + EPS)
        bias = total * jnp.concatenate([scale] * heads, axis=0)
        bias_ref[w, pl.ds(0, lines)] = bias[:, :key_len]
        bias_ref[w, pl.ds(lines, lines)] = bias[:, key_len:]

    for g in range(groups):
        pair_copies[g].wait()

        def pair_step(i, carry, g=g):
            pair_window(g * per_group + 2 * i)
            pair_window(g * per_group + 2 * i + 1)
            return carry

        lax.fori_loop(0, per_group // 2, pair_step, 0)

    for copy in loads[len(early) :]:
        copy.wait()
    for copy in copies:
        copy.wait()
    lanes = 128

    def as_row(ref):
        return ref[...].reshape(1, atoms)

    mask_ext = jnp.concatenate(
        [as_row(halo_m[0])[:, atoms - lanes :], as_row(mask_ref), as_row(halo_m[1])[:, :lanes]],
        axis=1,
    )
    token_ext = jnp.concatenate(
        [as_row(halo_t[0])[:, atoms - lanes :], as_row(token_ref), as_row(halo_t[1])[:, :lanes]],
        axis=1,
    )
    extent = atoms + 2 * lanes
    position = me * atoms - lanes + iota((1, extent), 1)
    usable = (
        (mask_ext == 1)
        & (position >= 0)
        & (position < n * atoms)
        & (position < count_ref[0])
    )
    live = jnp.broadcast_to(jnp.where(usable, 1.0, 0.0), (8, extent))
    for w in range(windows):
        shift = (extent - (lanes - margin + query_len * w)) % extent
        live_ref[w] = pltpu.roll(live, shift, axis=1)[:, :key_len]
    relative = jnp.where(usable, token_ext - me * tokens, -2)
    hits = iota((tokens, extent), 0) == jnp.broadcast_to(relative, (tokens, extent))
    hits = jnp.where(hits, 1.0, 0.0)
    counts_ref[...] = jnp.broadcast_to(
        1.0 / jnp.maximum(jnp.sum(hits, axis=1, keepdims=True), 1.0), counts_ref.shape
    )
    onehot_ref[...] = hits[:, lanes : lanes + atoms].astype(BF16)
    relative8 = jnp.broadcast_to(relative[:, lanes : lanes + atoms], (8, atoms))
    rolled8 = pltpu.roll(relative8, query_len, axis=1)
    lower_hit = jnp.where(relative8[:, :lanes] == -1, 1.0, 0.0).astype(BF16)[:, :query_len]
    upper_hit = jnp.where(rolled8[:, :lanes] == tokens, 1.0, 0.0).astype(BF16)[:, :query_len]

    for side in range(2):
        inside = (me > 0) if side == 0 else (me < n - 1)
        cond_halo = norm(halo_c[side]).astype(BF16)
        adapt = mm(cond_halo, ada_ref[0])
        scale = jax.nn.sigmoid(adapt[:, :width] + ada_bias_ref[0:1])
        shift = adapt[:, width:]
        normed = norm(halo_x[side].reshape(samples * margin, width))
        attn_in = (normed.reshape(samples, margin, width) * scale[None] + shift[None]).astype(BF16)
        projected = mm(
            attn_in.reshape(samples * margin, width), qkvg_ref[:, pl.ds(width, 2 * width)]
        )
        projected = jnp.where(inside, projected, 0.0).astype(BF16)
        start = 0 if side == 0 else margin + atoms
        kv_ref[:, pl.ds(start, margin), pl.ds(0, 2 * width)] = projected.reshape(
            samples, margin, 2 * width
        )

    head_of = iota((half, width), 1) // head_dim

    def attend(s, w):
        rows = pl.ds(pl.multiple_of(w * query_len, query_len), query_len)
        keys = pl.ds(pl.multiple_of(w * query_len, query_len), key_len)
        query = q_ref[s, rows]
        parts = []
        for side in range(2):
            piece = query[side * half : (side + 1) * half]
            for h in range(heads):
                parts.append(jnp.where(head_of == h, piece, jnp.zeros_like(piece)))
        stacked = jnp.concatenate(parts, axis=0)
        scores = lax.dot_general(
            stacked,
            kv_ref[s, keys, pl.ds(0, width)],
            (((1,), (1,)), ((), ())),
            preferred_element_type=F32,
        )
        scores = jnp.where(live_ref[w][0:1] > 0.5, scores + bias_ref[w], DEAD)
        top = jnp.max(scores, axis=1, keepdims=True)
        weights = jnp.exp(scores - top).astype(BF16)
        mixed = mm(weights, kv_ref[s, keys, pl.ds(width, 2 * width)])
        outs = []
        for side in range(2):
            base = side * heads * half
            value = mixed[base : base + half, :width]
            amount = mixed[base : base + half, width:]
            for h in range(1, heads):
                at = base + h * half
                value = jnp.where(head_of == h, mixed[at : at + half, :width], value)
                amount = jnp.where(head_of == h, mixed[at : at + half, width:], amount)
            outs.append(value / amount)
        return (jnp.concatenate(outs, axis=0) * gate_ref[s, rows]).astype(BF16)

    def process(pairs):
        rows = [pl.ds(pl.multiple_of(w * query_len, query_len), query_len) for w in pairs]
        order = [(s, i) for s in range(samples) for i in range(len(pairs))]

        def modulation(k):
            one = jnp.concatenate([mod_ref[k, r] for r in rows], axis=0)
            return jnp.concatenate([one] * samples, axis=0)

        blended = jnp.concatenate([attend(s, pairs[i]) for s, i in order], axis=0)
        stream = jnp.concatenate([atoms_ref[s, rows[i]] for s, i in order], axis=0).astype(F32)
        after = (stream + modulation(2) * mm(blended, out_ref[...])).astype(BF16)
        trans_in = (norm(after) * modulation(3) + modulation(4)).astype(BF16)
        mixed = mm(trans_in, swiglu_ref[...])
        units = (jax.nn.silu(mixed[:, :hidden]) * mixed[:, hidden:]).astype(BF16)
        final = (after.astype(F32) + modulation(5) * mm(units, down_ref[...])).astype(BF16)
        features = jnp.maximum(mm(final, token_weight_ref[...]), 0.0).astype(BF16)
        for place, (s, i) in enumerate(order):
            at = place * query_len
            atoms_out_ref[s, rows[i]] = final[at : at + query_len]
            feat_ref[s, rows[i]] = features[at : at + query_len]
        return features

    features = process([0, windows - 1])
    sample_row = iota((8, token_width), 0)
    for side, hit in enumerate((upper_hit, lower_hit)):
        place = 1 - side
        total = jnp.zeros((8, token_width), F32)
        for s in range(samples):
            at = (2 * s + place) * query_len
            total = jnp.where(sample_row == s, mm(hit, features[at : at + query_len]), total)
        edge_out[side] = total
    edge_copies = []
    for side, target in enumerate((right, left)):
        copy = pltpu.make_async_remote_copy(
            src_ref=edge_out.at[side],
            dst_ref=edge_in.at[side],
            send_sem=edge_send_sem.at[side],
            recv_sem=edge_recv_sem.at[side],
            device_id={"atom": target},
            device_id_type=MESH,
        )
        copy.start()
        edge_copies.append(copy)

    def middle(i, carry):
        process([per_step * i + 1 + j for j in range(per_step)])
        return carry

    per_step = (windows - 2) // STEPS
    lax.fori_loop(0, STEPS, middle, 0)

    for copy in edge_copies:
        copy.wait()
    token_row = iota((tokens, token_width), 0)
    per_count = counts_ref[:, 0:1]
    for s in range(samples):
        total = mm(onehot_ref[...], feat_ref[s])
        from_left = jnp.where(me > 0, edge_in[0, s : s + 1], 0.0)
        from_right = jnp.where(me < n - 1, edge_in[1, s : s + 1], 0.0)
        total = total + jnp.where(token_row == 0, from_left, 0.0)
        total = total + jnp.where(token_row == tokens - 1, from_right, 0.0)
        tokens_out_ref[s] = (total * per_count).astype(BF16)


def on_device(
    n,
    atoms_in, cond, pair, atom_mask, atom_count, atom_to_token, ada_weight, ada_bias,
    zero_weight, zero_bias, qkvg_weight, query_bias, pair_weight, out_weight,
    swiglu_weight, down_weight, token_weight,
):
    samples, atoms, width = atoms_in.shape
    windows, query_len, channels, key_len = pair.shape
    heads = pair_weight.shape[0]
    margin = (key_len - query_len) // 2
    tokens = atoms // ATOMS_PER_TOKEN
    token_width = token_weight.shape[1]
    half = query_len // 2
    rows_half = half * channels
    groups = 3 if windows % 6 == 0 else 1
    vmem = pl.BlockSpec(memory_space=pltpu.VMEM)
    hbm = pl.BlockSpec(memory_space=pltpu.HBM)
    query_bias = query_bias.reshape(1, width)
    staged = (
        atoms_in, cond, ada_weight, ada_bias, zero_weight, zero_bias, qkvg_weight,
        query_bias, pair_weight, out_weight, swiglu_weight, down_weight, token_weight,
        atom_mask, atom_to_token,
    )
    smem = pl.BlockSpec(memory_space=pltpu.SMEM)
    return pl.pallas_call(
        functools.partial(block_body, n),
        out_shape=(
            pltpu.VMEM(atoms_in.shape, BF16),
            pltpu.VMEM((samples, tokens, token_width), BF16),
        ),
        in_specs=[hbm, hbm, hbm, hbm, hbm, smem] + [hbm] * 11,
        out_specs=(vmem, vmem),
        scratch_shapes=[pltpu.VMEM(a.shape, a.dtype) for a in staged]
        + [
            pltpu.VMEM((windows, query_len * channels, key_len), BF16),
            pltpu.VMEM((2, samples, margin, width), BF16),
            pltpu.VMEM((2, margin, width), BF16),
            pltpu.VMEM((atoms,), jnp.int32),
            pltpu.VMEM((atoms,), jnp.int32),
            pltpu.VMEM((atoms,), jnp.int32),
            pltpu.VMEM((atoms,), jnp.int32),
            pltpu.VMEM((samples, atoms + 2 * margin, 3 * width), BF16),
            pltpu.VMEM((samples, atoms, width), BF16),
            pltpu.VMEM((samples, atoms, width), F32),
            pltpu.VMEM((windows, heads * query_len, key_len), F32),
            pltpu.VMEM((windows, 8, key_len), F32),
            pltpu.VMEM((6, atoms, width), F32),
            pltpu.VMEM((samples, atoms, token_width), BF16),
            pltpu.VMEM((width, width), BF16),
            pltpu.VMEM((2 * width, width), BF16),
            pltpu.VMEM((rows_half + 3 * heads * half, rows_half), BF16),
            pltpu.VMEM((half, rows_half), BF16),
            pltpu.VMEM((2, 8, token_width), F32),
            pltpu.VMEM((2, 8, token_width), F32),
            pltpu.VMEM((tokens, atoms), BF16),
            pltpu.VMEM((tokens, 128), F32),
            pltpu.SemaphoreType.DMA((len(staged),)),
            pltpu.SemaphoreType.DMA((groups,)),
            pltpu.SemaphoreType.DMA((2, 4)),
            pltpu.SemaphoreType.DMA((2, 4)),
            pltpu.SemaphoreType.DMA((2,)),
            pltpu.SemaphoreType.DMA((2,)),
        ],
        compiler_params=pltpu.CompilerParams(collective_id=0, has_side_effects=True),
        name="atom_block",
    )(
        atoms_in, cond, pair.reshape(windows, query_len * channels, key_len),
        atom_mask, atom_to_token, atom_count,
        ada_weight, ada_bias, zero_weight, zero_bias, qkvg_weight,
        query_bias, pair_weight, out_weight, swiglu_weight,
        down_weight, token_weight,
    )


def solution(mesh):
    shard = P(("struct", "atom"))
    stream = P("struct", "atom", None)
    in_specs = (stream, shard, shard, shard, P("struct"), shard) + (P(),) * 11
    return jax.shard_map(
        functools.partial(on_device, mesh.shape["atom"]),
        mesh=mesh,
        in_specs=in_specs,
        out_specs=(stream, stream),
        check_vma=False,
    )
```

profile of v0, /device:TPU:1, one launch (start us, length us, event | category | flops | bytes accessed | tf_op | source)
XLA Modules:
  0.0 26.2 jit_solution(1856213757649801042)
XLA Ops:
  1.3 23.4 %atom_block.1 = (bf16[4,384,128]{2,1,0:T(8,128)(2,1)S(1)}, bf16[4,48,768]{2,1,0:T(8,128)(2,1)S(1)}) custom-call(bf16[4,384,128]{2,1,0:T(8,128)(2,1)} %atoms_hbm.1, bf16[384,128]{1,0:T(8,128)(2,1)} %cond_hbm.1, bf16[12,512,128]{2,1,0:T(8,128)(2,1)} %bitcast.2, s32[384]{0:T(512)} %mask_hbm.1, s32[384]{0:T(512)} %token_hbm.1, s32[1]{0:T(128)S(6)} %copy.23.count_ref, ...), custom_call_target="tpu_custom_call" | custom-call | tf_op jit(solution)/shard_map/atom_block/pallas_call | solution.py:392
  24.7 0.7 %copy.21 = bf16[4,384,128]{2,1,0:T(8,128)(2,1)} copy(bf16[4,384,128]{2,1,0:T(8,128)(2,1)S(1)} %get-tuple-element.2) | data formatting | bytes 786432
  25.5 0.7 %copy.22 = bf16[4,48,768]{2,1,0:T(8,128)(2,1)} copy(bf16[4,48,768]{2,1,0:T(8,128)(2,1)S(1)} %get-tuple-element.3) | data formatting | bytes 589824
where the time goes:
time: 26.3 us; the launch traced here: 26.2 us
  Pallas kernels  23.4 us (89%)
  local copies, waits for them, and re-layouts  1.46 us (6%)
  between operations  1.29 us (5%)
    pallas_call x1, Pallas kernels, on_device(): pl.pallas_call(functools.partial(block_body, n), out_shape=(pltpu.VMEM(at...  23.4 us
    unnamed x2, local copies, waits for them, and re-layouts  1.46 us

commit v1 on v0

--- a/solution.py
+++ b/solution.py
@@ -9,8 +9,9 @@
 
 ATOMS_PER_TOKEN = 8
 EPS = 1e-05
-STEPS = 1
-DEAD = -1000000000.0
+DEAD = -1e30
+MIX_LAG = 2
+BLEND_LAG = 1
 MESH = pl.DeviceIdType.MESH
 F32 = jnp.float32
 BF16 = jnp.bfloat16
@@ -40,7 +41,7 @@
     query_bias_ref, pair_weight_ref, out_ref, swiglu_ref, down_ref, token_weight_ref,
     mask_ref, token_ref,
     pair_buf, halo_x, halo_c, halo_m0, halo_m1, halo_t0, halo_t1, kv_ref, q_ref, gate_ref, bias_ref,
-    live_ref, mod_ref, feat_ref, center_ref, mean_ref, lhs_ref, fold_ref,
+    mod_ref, feat_ref, blend_ref, center_ref, mean_ref, lhs_ref,
     edge_out, edge_in, onehot_ref, counts_ref,
     load_sem, pair_sem, send_sem, recv_sem, edge_send_sem, edge_recv_sem,
 ):
@@ -68,11 +69,11 @@
         (cond_hbm, cond_ref), (atoms_hbm, atoms_ref), (ada_hbm, ada_ref),
         (ada_bias_hbm, ada_bias_ref), (zero_hbm, zero_ref), (zero_bias_hbm, zero_bias_ref),
         (qkvg_hbm, qkvg_ref), (query_bias_hbm, query_bias_ref),
-        (pair_weight_hbm, pair_weight_ref),
+        (pair_weight_hbm, pair_weight_ref), (mask_hbm, mask_ref), (token_hbm, token_ref),
     )
     late = (
         (out_hbm, out_ref), (swiglu_hbm, swiglu_ref), (down_hbm, down_ref),
-        (token_weight_hbm, token_weight_ref), (mask_hbm, mask_ref), (token_hbm, token_ref),
+        (token_weight_hbm, token_weight_ref),
     )
     loads = [
         pltpu.make_async_copy(src, dst, load_sem.at[i])
@@ -97,14 +98,12 @@
     mean_ref[...] = jnp.full(mean_ref.shape, inverse, F32).astype(BF16)
     kv_ref[:, :, 2 * width :] = jnp.ones((samples, atoms + 2 * margin, width), BF16)
     row, col = iota((rows_half, rows_half), 0), iota((rows_half, rows_half), 1)
-    same = jnp.where(row // channels == col // channels, 1.0 / channels, 0.0)
-    lhs_ref[pl.ds(0, rows_half)] = (jnp.where(row == col, 1.0, 0.0) - same).astype(BF16)
-    folded = rows_half // 2
-    fold_ref[...] = jnp.where(
-        (iota((half, 2 * folded), 1) % folded) // (channels // 2) == iota((half, 2 * folded), 0),
-        1.0 / channels,
-        0.0,
-    ).astype(BF16)
+    place = (row % half) * channels + row // half
+    same = jnp.where(row % half == col // channels, 1.0 / channels, 0.0)
+    lhs_ref[pl.ds(0, rows_half)] = (jnp.where(place == col, 1.0, 0.0) - same).astype(BF16)
+
+    for copy in loads[: len(early)]:
+        copy.wait()
 
     pl.semaphore_wait(barrier, 2)
 
@@ -113,10 +112,10 @@
         own = pl.ds(start, margin)
         for which, (src, dst) in enumerate(
             (
-                (atoms_hbm.at[:, own], halo_x.at[side]),
-                (cond_hbm.at[own], halo_c.at[side]),
-                (mask_hbm, halo_m[side]),
-                (token_hbm, halo_t[side]),
+                (atoms_ref.at[:, own], halo_x.at[side]),
+                (cond_ref.at[own], halo_c.at[side]),
+                (mask_ref, halo_m[side]),
+                (token_ref, halo_t[side]),
             )
         ):
             copy = pltpu.make_async_remote_copy(
@@ -130,29 +129,33 @@
             copy.start()
             copies.append(copy)
 
-    for copy in loads[: len(early)]:
-        copy.wait()
-
-    def norm(values):
-        centred = mm(values, center_ref[...])
+    def centre(values):
+        return mm(values, center_ref[...])
+
+    def scaled(centred):
         high, low = two_pieces(centred * centred)
         spread = mm(jnp.concatenate([high, low], axis=1), mean_ref[...])
         return centred * lax.rsqrt(spread + EPS)
 
-    cond_norm = norm(cond_ref[...]).astype(BF16)
+    cond_centred = centre(cond_ref[...])
+    atom_centred = [centre(atoms_ref[s]) for s in range(samples)]
+    cond_norm = scaled(cond_centred).astype(BF16)
+    normed = [scaled(c) for c in atom_centred]
     for which in range(2):
         adapt = mm(cond_norm, ada_ref[which])
         mod_ref[3 * which] = jax.nn.sigmoid(
             adapt[:, :width] + ada_bias_ref[which : which + 1]
         )
         mod_ref[3 * which + 1] = adapt[:, width:]
+    zeroed = mm(cond_norm, jnp.concatenate([zero_ref[0], zero_ref[1]], axis=1))
+    for which in range(2):
         mod_ref[3 * which + 2] = jax.nn.sigmoid(
-            mm(cond_norm, zero_ref[which]) + zero_bias_ref[which : which + 1]
+            zeroed[:, which * width : (which + 1) * width] + zero_bias_ref[which : which + 1]
         )
 
     factor = head_dim**-0.5
     for s in range(samples):
-        attn_in = (norm(atoms_ref[s]) * mod_ref[0] + mod_ref[1]).astype(BF16)
+        attn_in = (normed[s] * mod_ref[0] + mod_ref[1]).astype(BF16)
         projected = mm(attn_in, qkvg_ref[...])
         q_ref[s] = ((projected[:, :width] + query_bias_ref[...]) * factor).astype(BF16)
         kv_ref[s, pl.ds(margin, atoms), pl.ds(0, 2 * width)] = projected[
@@ -179,35 +182,52 @@
         lhs_ref[pl.ds(rows_half + piece * lines, lines)] = jnp.concatenate(
             blocks, axis=0
         ).astype(BF16)
-    def pair_window(w):
+
+    def pair_window(w, live):
         block = pair_buf[w]
         both = jnp.concatenate([block[:rows_half], block[rows_half:]], axis=1)
         result = mm(lhs_ref[...], both)
-        centred = result[:rows_half]
+        square = None
+        for c in range(channels):
+            centred = result[c * half : (c + 1) * half]
+            square = centred * centred if c == 0 else square + centred * centred
         at = rows_half
         total = (
             result[at : at + lines]
             + result[at + lines : at + 2 * lines]
             + result[at + 2 * lines : at + 3 * lines]
         )
-        square = (centred * centred).reshape(half, 2, channels // 2, 2 * key_len)
-        square = (square[:, 0] + square[:, 1]).reshape(folded, 2 * key_len)
-        high, low = two_pieces(square)
-        spread = mm(fold_ref[...], jnp.concatenate([high, low], axis=0))
-        scale = lax.rsqrt(spread + EPS)
+        scale = lax.rsqrt(square * (1.0 / channels) + EPS)
         bias = total * jnp.concatenate([scale] * heads, axis=0)
+        keep = jnp.concatenate([live, live], axis=1)[0:1] > 0.5
+        bias = jnp.where(keep, bias, DEAD)
         bias_ref[w, pl.ds(0, lines)] = bias[:, :key_len]
         bias_ref[w, pl.ds(lines, lines)] = bias[:, key_len:]
 
-    for g in range(groups):
-        pair_copies[g].wait()
-
-        def pair_step(i, carry, g=g):
-            pair_window(g * per_group + 2 * i)
-            pair_window(g * per_group + 2 * i + 1)
-            return carry
-
-        lax.fori_loop(0, per_group // 2, pair_step, 0)
+    def as_row(ref):
+        return ref[...].reshape(1, atoms)
+
+    def usable_at(mask, position):
+        return (
+            (mask == 1)
+            & (position >= 0)
+            & (position < n * atoms)
+            & (position < count_ref[0])
+        )
+
+    inner = [
+        w
+        for w in range(windows)
+        if w * query_len >= margin and w * query_len - margin + key_len <= atoms
+    ]
+    outer = [w for w in range(windows) if w not in inner]
+    usable = usable_at(as_row(mask_ref), me * atoms + iota((1, atoms), 1))
+    live = jnp.broadcast_to(jnp.where(usable, 1.0, 0.0), (8, atoms))
+    for copy in pair_copies:
+        copy.wait()
+    for w in inner:
+        start = w * query_len - margin
+        pair_window(w, pltpu.roll(live, (atoms - start) % atoms, axis=1)[:, :key_len])
 
     for copy in loads[len(early) :]:
         copy.wait()
@@ -215,8 +235,10 @@
         copy.wait()
     lanes = 128
 
-    def as_row(ref):
-        return ref[...].reshape(1, atoms)
+    halo_centred = [
+        centre(ref[...])
+        for ref in (halo_c.at[0], halo_c.at[1])
+    ] + [centre(halo_x[side].reshape(samples * margin, width)) for side in range(2)]
 
     mask_ext = jnp.concatenate(
         [as_row(halo_m[0])[:, atoms - lanes :], as_row(mask_ref), as_row(halo_m[1])[:, :lanes]],
@@ -227,17 +249,38 @@
         axis=1,
     )
     extent = atoms + 2 * lanes
-    position = me * atoms - lanes + iota((1, extent), 1)
-    usable = (
-        (mask_ext == 1)
-        & (position >= 0)
-        & (position < n * atoms)
-        & (position < count_ref[0])
-    )
+    usable = usable_at(mask_ext, me * atoms - lanes + iota((1, extent), 1))
     live = jnp.broadcast_to(jnp.where(usable, 1.0, 0.0), (8, extent))
-    for w in range(windows):
+
+    def outer_pair(w):
         shift = (extent - (lanes - margin + query_len * w)) % extent
-        live_ref[w] = pltpu.roll(live, shift, axis=1)[:, :key_len]
+        pair_window(w, pltpu.roll(live, shift, axis=1)[:, :key_len])
+
+    pending = list(outer)
+    if pending:
+        outer_pair(pending.pop(0))
+    halo_normed = [scaled(c) for c in halo_centred]
+    if pending:
+        outer_pair(pending.pop(0))
+    halo_adapt = [mm(halo_normed[side].astype(BF16), ada_ref[0]) for side in range(2)]
+    while pending:
+        outer_pair(pending.pop(0))
+    for side in range(2):
+        inside = (me > 0) if side == 0 else (me < n - 1)
+        scale = jax.nn.sigmoid(halo_adapt[side][:, :width] + ada_bias_ref[0:1])
+        shift = halo_adapt[side][:, width:]
+        attn_in = (
+            halo_normed[2 + side].reshape(samples, margin, width) * scale[None] + shift[None]
+        ).astype(BF16)
+        projected = mm(
+            attn_in.reshape(samples * margin, width), qkvg_ref[:, pl.ds(width, 2 * width)]
+        )
+        projected = jnp.where(inside, projected, 0.0).astype(BF16)
+        start = 0 if side == 0 else margin + atoms
+        kv_ref[:, pl.ds(start, margin), pl.ds(0, 2 * width)] = projected.reshape(
+            samples, margin, 2 * width
+        )
+
     relative = jnp.where(usable, token_ext - me * tokens, -2)
     hits = iota((tokens, extent), 0) == jnp.broadcast_to(relative, (tokens, extent))
     hits = jnp.where(hits, 1.0, 0.0)
@@ -250,107 +293,140 @@
     lower_hit = jnp.where(relative8[:, :lanes] == -1, 1.0, 0.0).astype(BF16)[:, :query_len]
     upper_hit = jnp.where(rolled8[:, :lanes] == tokens, 1.0, 0.0).astype(BF16)[:, :query_len]
 
-    for side in range(2):
-        inside = (me > 0) if side == 0 else (me < n - 1)
-        cond_halo = norm(halo_c[side]).astype(BF16)
-        adapt = mm(cond_halo, ada_ref[0])
-        scale = jax.nn.sigmoid(adapt[:, :width] + ada_bias_ref[0:1])
-        shift = adapt[:, width:]
-        normed = norm(halo_x[side].reshape(samples * margin, width))
-        attn_in = (normed.reshape(samples, margin, width) * scale[None] + shift[None]).astype(BF16)
-        projected = mm(
-            attn_in.reshape(samples * margin, width), qkvg_ref[:, pl.ds(width, 2 * width)]
-        )
-        projected = jnp.where(inside, projected, 0.0).astype(BF16)
-        start = 0 if side == 0 else margin + atoms
-        kv_ref[:, pl.ds(start, margin), pl.ds(0, 2 * width)] = projected.reshape(
-            samples, margin, 2 * width
-        )
-
     head_of = iota((half, width), 1) // head_dim
-
-    def attend(s, w):
-        rows = pl.ds(pl.multiple_of(w * query_len, query_len), query_len)
-        keys = pl.ds(pl.multiple_of(w * query_len, query_len), key_len)
-        query = q_ref[s, rows]
+    blank = jnp.zeros((key_len, width), BF16)
+
+    def stacked(s, w):
+        query = q_ref[s, pl.ds(w * query_len, query_len)]
         parts = []
         for side in range(2):
             piece = query[side * half : (side + 1) * half]
             for h in range(heads):
                 parts.append(jnp.where(head_of == h, piece, jnp.zeros_like(piece)))
-        stacked = jnp.concatenate(parts, axis=0)
+        return jnp.concatenate(parts, axis=0)
+
+    def score(w, group):
+        keys = pl.ds(w * query_len, key_len)
+        bias = bias_ref[w]
+        both = jnp.concatenate([stacked(s, w) for s in group], axis=1)
+        tall = jnp.concatenate(
+            [
+                jnp.concatenate(
+                    [kv_ref[s, keys, pl.ds(0, width)] if t == s else blank for t in group], axis=1
+                )
+                for s in group
+            ],
+            axis=0,
+        )
         scores = lax.dot_general(
-            stacked,
-            kv_ref[s, keys, pl.ds(0, width)],
-            (((1,), (1,)), ((), ())),
-            preferred_element_type=F32,
-        )
-        scores = jnp.where(live_ref[w][0:1] > 0.5, scores + bias_ref[w], DEAD)
-        top = jnp.max(scores, axis=1, keepdims=True)
-        weights = jnp.exp(scores - top).astype(BF16)
-        mixed = mm(weights, kv_ref[s, keys, pl.ds(width, 2 * width)])
-        outs = []
-        for side in range(2):
-            base = side * heads * half
-            value = mixed[base : base + half, :width]
-            amount = mixed[base : base + half, width:]
-            for h in range(1, heads):
-                at = base + h * half
-                value = jnp.where(head_of == h, mixed[at : at + half, :width], value)
-                amount = jnp.where(head_of == h, mixed[at : at + half, width:], amount)
-            outs.append(value / amount)
-        return (jnp.concatenate(outs, axis=0) * gate_ref[s, rows]).astype(BF16)
-
-    def process(pairs):
-        rows = [pl.ds(pl.multiple_of(w * query_len, query_len), query_len) for w in pairs]
-        order = [(s, i) for s in range(samples) for i in range(len(pairs))]
+            both, tall, (((1,), (1,)), ((), ())), preferred_element_type=F32
+        )
+        found = []
+        for i in range(len(group)):
+            own = scores[:, i * key_len : (i + 1) * key_len] + bias
+            found.append((own, jnp.max(own, axis=1, keepdims=True)))
+        return found
+
+    def mix(w, group, found):
+        keys = pl.ds(w * query_len, key_len)
+        return [
+            mm(jnp.exp(own - top).astype(BF16), kv_ref[s, keys, pl.ds(width, 2 * width)])
+            for s, (own, top) in zip(group, found)
+        ]
+
+    def blend(w, group, mixes):
+        rows = pl.ds(w * query_len, query_len)
+        for s, mixed in zip(group, mixes):
+            outs = []
+            for side in range(2):
+                base = side * heads * half
+                value = mixed[base : base + half, :width]
+                amount = mixed[base : base + half, width:]
+                for h in range(1, heads):
+                    at = base + h * half
+                    value = jnp.where(head_of == h, mixed[at : at + half, :width], value)
+                    amount = jnp.where(head_of == h, mixed[at : at + half, width:], amount)
+                outs.append(value / amount)
+            blend_ref[s, rows] = (jnp.concatenate(outs, axis=0) * gate_ref[s, rows]).astype(BF16)
+
+    def transition(parts):
+        def gather(ref):
+            return jnp.concatenate([ref[s, pl.ds(a, m)] for s, a, m in parts], axis=0)
 
         def modulation(k):
-            one = jnp.concatenate([mod_ref[k, r] for r in rows], axis=0)
-            return jnp.concatenate([one] * samples, axis=0)
-
-        blended = jnp.concatenate([attend(s, pairs[i]) for s, i in order], axis=0)
-        stream = jnp.concatenate([atoms_ref[s, rows[i]] for s, i in order], axis=0).astype(F32)
-        after = (stream + modulation(2) * mm(blended, out_ref[...])).astype(BF16)
-        trans_in = (norm(after) * modulation(3) + modulation(4)).astype(BF16)
+            return jnp.concatenate([mod_ref[k, pl.ds(a, m)] for _, a, m in parts], axis=0)
+
+        mixed = mm(gather(blend_ref), out_ref[...])
+        yield
+        after = (gather(atoms_ref).astype(F32) + modulation(2) * mixed).astype(BF16)
+        centred = centre(after)
+        yield
+        trans_in = scaled(centred)
+        yield
+        trans_in = (trans_in * modulation(3) + modulation(4)).astype(BF16)
         mixed = mm(trans_in, swiglu_ref[...])
+        yield
         units = (jax.nn.silu(mixed[:, :hidden]) * mixed[:, hidden:]).astype(BF16)
-        final = (after.astype(F32) + modulation(5) * mm(units, down_ref[...])).astype(BF16)
+        mixed = mm(units, down_ref[...])
+        yield
+        final = (after.astype(F32) + modulation(5) * mixed).astype(BF16)
         features = jnp.maximum(mm(final, token_weight_ref[...]), 0.0).astype(BF16)
-        for place, (s, i) in enumerate(order):
-            at = place * query_len
-            atoms_out_ref[s, rows[i]] = final[at : at + query_len]
-            feat_ref[s, rows[i]] = features[at : at + query_len]
-        return features
-
-    features = process([0, windows - 1])
-    sample_row = iota((8, token_width), 0)
-    for side, hit in enumerate((upper_hit, lower_hit)):
-        place = 1 - side
-        total = jnp.zeros((8, token_width), F32)
-        for s in range(samples):
-            at = (2 * s + place) * query_len
-            total = jnp.where(sample_row == s, mm(hit, features[at : at + query_len]), total)
-        edge_out[side] = total
+        at = 0
+        for s, a, m in parts:
+            atoms_out_ref[s, pl.ds(a, m)] = final[at : at + m]
+            feat_ref[s, pl.ds(a, m)] = features[at : at + m]
+            at += m
+        yield
+
     edge_copies = []
-    for side, target in enumerate((right, left)):
-        copy = pltpu.make_async_remote_copy(
-            src_ref=edge_out.at[side],
-            dst_ref=edge_in.at[side],
-            send_sem=edge_send_sem.at[side],
-            recv_sem=edge_recv_sem.at[side],
-            device_id={"atom": target},
-            device_id_type=MESH,
-        )
-        copy.start()
-        edge_copies.append(copy)
-
-    def middle(i, carry):
-        process([per_step * i + 1 + j for j in range(per_step)])
-        return carry
-
-    per_step = (windows - 2) // STEPS
-    lax.fori_loop(0, STEPS, middle, 0)
+
+    def edges():
+        last = atoms - query_len
+        parts = [(s, a, query_len) for s in range(samples) for a in (0, last)]
+        yield from transition(parts)
+        sample_row = iota((8, token_width), 0)
+        for side, hit in enumerate((upper_hit, lower_hit)):
+            total = jnp.zeros((8, token_width), F32)
+            for s in range(samples):
+                rows = pl.ds(last if side == 0 else 0, query_len)
+                total = jnp.where(sample_row == s, mm(hit, feat_ref[s, rows]), total)
+            edge_out[side] = total
+        for side, target in enumerate((right, left)):
+            copy = pltpu.make_async_remote_copy(
+                src_ref=edge_out.at[side],
+                dst_ref=edge_in.at[side],
+                send_sem=edge_send_sem.at[side],
+                recv_sem=edge_recv_sem.at[side],
+                device_id={"atom": target},
+                device_id_type=MESH,
+            )
+            copy.start()
+            edge_copies.append(copy)
+        yield
+
+    ends = [0, windows - 1]
+    order = ends + [w for w in range(windows) if w not in ends]
+    units = [(w, (s, s + 1)) for w in order for s in range(0, samples, 2)]
+    ready = len(ends) * samples // 2
+    found, mixes = {}, {}
+    edge_steps = edges()
+    for i in range(len(units) + MIX_LAG + BLEND_LAG):
+        if i < len(units):
+            found[i] = score(*units[i])
+        j = i - MIX_LAG
+        if 0 <= j < len(units):
+            mixes[j] = mix(*units[j], found.pop(j))
+        j = j - BLEND_LAG
+        if 0 <= j < len(units):
+            blend(*units[j], mixes.pop(j))
+        if j >= ready:
+            next(edge_steps, None)
+    for _ in edge_steps:
+        pass
+
+    middle = [(s, query_len, atoms - 2 * query_len) for s in range(samples)]
+    for _ in transition(middle):
+        pass
 
     for copy in edge_copies:
         copy.wait()
@@ -410,13 +486,12 @@
             pltpu.VMEM((samples, atoms, width), BF16),
             pltpu.VMEM((samples, atoms, width), F32),
             pltpu.VMEM((windows, heads * query_len, key_len), F32),
-            pltpu.VMEM((windows, 8, key_len), F32),
             pltpu.VMEM((6, atoms, width), F32),
             pltpu.VMEM((samples, atoms, token_width), BF16),
+            pltpu.VMEM((samples, atoms, width), BF16),
             pltpu.VMEM((width, width), BF16),
             pltpu.VMEM((2 * width, width), BF16),
             pltpu.VMEM((rows_half + 3 * heads * half, rows_half), BF16),
-            pltpu.VMEM((half, rows_half), BF16),
             pltpu.VMEM((2, 8, token_width), F32),
             pltpu.VMEM((2, 8, token_width), F32),
             pltpu.VMEM((tokens, atoms), BF16),

time: 26.3 us -> 14.9 us (0.57)
  Pallas kernels: 23.4 us -> 11.9 us
    pallas_call x1, Pallas kernels: 23.4 us -> 11.9 us  [on_device(): pl.pallas_call(functools.partial(block_body, n), out_shape=(pltpu.VMEM(at...]
where the time goes in v1:
time: 14.9 us; the launch traced here: 14.7 us
  Pallas kernels  11.9 us (80%)
  local copies, waits for them, and re-layouts  1.46 us (10%)
  between operations  1.29 us (9%)
    pallas_call x1, Pallas kernels, on_device(): pl.pallas_call(functools.partial(block_body, n), out_shape=(pltpu.VMEM(at...  11.9 us
    unnamed x2, local copies, waits for them, and re-layouts  1.46 us

profile of v1, /device:TPU:1, one launch (start us, length us, event | category | flops | bytes accessed | tf_op | source)
XLA Modules:
  0.0 14.7 jit_solution(6476405397728052398)
XLA Ops:
  1.3 11.9 %atom_block.1 = (bf16[4,384,128]{2,1,0:T(8,128)(2,1)S(1)}, bf16[4,48,768]{2,1,0:T(8,128)(2,1)S(1)}) custom-call(bf16[4,384,128]{2,1,0:T(8,128)(2,1)} %atoms_hbm.1, bf16[384,128]{1,0:T(8,128)(2,1)} %cond_hbm.1, bf16[12,512,128]{2,1,0:T(8,128)(2,1)} %bitcast.2, s32[384]{0:T(512)} %mask_hbm.1, s32[384]{0:T(512)} %token_hbm.1, s32[1]{0:T(128)S(6)} %copy.23.count_ref, ...), custom_call_target="tpu_custom_call" | custom-call | tf_op jit(solution)/shard_map/atom_block/pallas_call | solution.py:468
  13.2 0.7 %copy.21 = bf16[4,384,128]{2,1,0:T(8,128)(2,1)} copy(bf16[4,384,128]{2,1,0:T(8,128)(2,1)S(1)} %get-tuple-element.2) | data formatting | bytes 786432
  14.0 0.7 %copy.22 = bf16[4,48,768]{2,1,0:T(8,128)(2,1)} copy(bf16[4,48,768]{2,1,0:T(8,128)(2,1)S(1)} %get-tuple-element.3) | data formatting | bytes 589824

commit v2 on v1

v2 whole, which is shorter than its diff:
```python
import functools

import jax
import jax.numpy as jnp
from jax import lax
from jax.experimental import pallas as pl
from jax.experimental.pallas import tpu as pltpu
from jax.sharding import PartitionSpec as P

ATOMS_PER_TOKEN = 8
EPS = 1e-05
DEAD = -1e30
MIX_LAG = 2
BLEND_LAG = 1
FILL_HALO = 2
FILL_EVERY = 2
MESH = pl.DeviceIdType.MESH
F32 = jnp.float32
BF16 = jnp.bfloat16


def iota(shape, axis):
    return lax.broadcasted_iota(jnp.int32, shape, axis)


def mm(a, b):
    return jnp.dot(a, b, preferred_element_type=F32)


def block_body(
    n,
    atoms_hbm, cond_hbm, pair_ref, mask_hbm, token_hbm, count_hbm,
    ada_hbm, ada_bias_hbm, zero_hbm, zero_bias_hbm, qkvg_hbm, query_bias_hbm,
    pair_weight_hbm, out_hbm, swiglu_hbm, down_hbm, token_weight_hbm,
    atoms_out_ref, tokens_out_ref,
    cond_ref, ada_ref, ada_bias_ref, zero_ref, zero_bias_ref, qkvg_ref,
    query_bias_ref, pair_weight_ref, out_ref, swiglu_ref, down_ref, token_weight_ref,
    mask_ref, token_ref, count_ref, atoms_ref,
    pair_buf, pair_far, halo_x, halo_c, halo_m0, halo_m1, halo_t0, halo_t1,
    kv_ref, q_ref, gate_ref, bias_ref, mod_ref, feat_ref, blend_ref, lhs_ref,
    load_sem, pair_sem, send_sem, recv_sem,
):
    samples, atoms, width = atoms_out_ref.shape
    windows, rows_pair, key_len = pair_ref.shape
    heads, channels = pair_weight_ref.shape
    head_dim = width // heads
    query_len = rows_pair // channels
    half = query_len // 2
    margin = (key_len - query_len) // 2
    wide = margin + query_len
    reach = ATOMS_PER_TOKEN
    tokens = tokens_out_ref.shape[1]
    hidden = down_ref.shape[0]
    rows_half = half * channels
    lines = heads * half
    lanes = 128

    halo_m, halo_t = (halo_m0, halo_m1), (halo_t0, halo_t1)
    me = lax.axis_index("atom")
    right, left = lax.rem(me + 1, n), lax.rem(me + n - 1, n)

    barrier = pltpu.get_barrier_semaphore()
    has_left, has_right = me > 0, me < n - 1

    @pl.when(has_left)
    def _():
        pl.semaphore_signal(barrier, inc=1, device_id={"atom": left}, device_id_type=MESH)

    @pl.when(has_right)
    def _():
        pl.semaphore_signal(barrier, inc=1, device_id={"atom": right}, device_id_type=MESH)


    early = (
        (cond_hbm, cond_ref), (atoms_hbm, atoms_ref.at[:, pl.ds(0, atoms)]), (ada_hbm, ada_ref),
        (ada_bias_hbm, ada_bias_ref), (zero_hbm, zero_ref), (zero_bias_hbm, zero_bias_ref),
        (qkvg_hbm, qkvg_ref), (query_bias_hbm, query_bias_ref),
        (pair_weight_hbm, pair_weight_ref), (mask_hbm, mask_ref), (token_hbm, token_ref),
        (count_hbm, count_ref),
    )
    late = (
        (out_hbm, out_ref), (swiglu_hbm, swiglu_ref), (down_hbm, down_ref),
        (token_weight_hbm, token_weight_ref),
    )
    loads = [
        pltpu.make_async_copy(src, dst, load_sem.at[i])
        for i, (src, dst) in enumerate(early + late)
    ]
    for copy in loads[: len(early)]:
        copy.start()
    pair_copies = [pltpu.make_async_copy(pair_ref, pair_buf, pair_sem.at[0])]
    pair_copies[0].start()
    for copy in loads[len(early) :]:
        copy.start()

    inverse = 1.0 / width
    kv_ref[:, :, 2 * width :] = jnp.ones((samples, atoms + 2 * wide, width), BF16)
    row, col = iota((rows_half, rows_half), 0), iota((rows_half, rows_half), 1)
    place = (row % half) * channels + row // half
    same = jnp.where(row % half == col // channels, 1.0 / channels, 0.0)
    lhs_ref[pl.ds(0, rows_half)] = (jnp.where(place == col, 1.0, 0.0) - same).astype(BF16)

    skipped = rows_half - reach * channels
    pair_far[pl.ds(0, skipped)] = jnp.zeros((skipped, key_len), BF16)
    pair_far[pl.ds(2 * rows_half - skipped, skipped)] = jnp.zeros((skipped, key_len), BF16)
    for side, there in enumerate((has_left, has_right)):

        @pl.when(jnp.logical_not(there))
        def _(side=side):
            at = skipped + side * reach * channels
            pair_far[pl.ds(at, reach * channels)] = jnp.zeros((reach * channels, key_len), BF16)
            halo_x[side] = jnp.zeros(halo_x.shape[1:], BF16)
            halo_c[side] = jnp.zeros(halo_c.shape[1:], BF16)
            halo_m[side][...] = jnp.zeros(halo_m0.shape, jnp.int32)
            halo_t[side][...] = jnp.zeros(halo_t0.shape, jnp.int32)

    copies = []
    for side, (target, start, far) in enumerate(
        ((right, atoms - wide, (windows - 1, rows_pair - reach * channels)), (left, 0, (0, 0)))
    ):
        own = pl.ds(start, wide)
        size = reach * channels
        for which, (src, dst) in enumerate(
            (
                (atoms_ref.at[:, own], halo_x.at[side]),
                (cond_ref.at[own], halo_c.at[side]),
                (mask_ref, halo_m[side]),
                (token_ref, halo_t[side]),
                (
                    pair_buf.at[far[0], pl.ds(far[1], size)],
                    pair_far.at[pl.ds(skipped + side * size, size)],
                ),
            )
        ):
            copies.append(
                pltpu.make_async_remote_copy(
                    src_ref=src,
                    dst_ref=dst,
                    send_sem=send_sem.at[side, which],
                    recv_sem=recv_sem.at[side, which],
                    device_id={"atom": target},
                    device_id_type=MESH,
                )
            )
    to_right, to_left = copies[:5], copies[5:]

    def sends(chosen):
        @pl.when(has_right)
        def _():
            for k in chosen:
                to_right[k].start()

        @pl.when(has_left)
        def _():
            for k in chosen:
                to_left[k].start()

    for copy in loads[: len(early)]:
        copy.wait()

    pl.semaphore_wait(barrier, (me + n - 1) // n + (2 * n - 2 - me) // n)

    sends(range(4))

    def norm(values):
        values = values.astype(F32)
        centred = values - jnp.sum(values, axis=1, keepdims=True) * inverse
        spread = jnp.sum(centred * centred, axis=1, keepdims=True) * inverse
        return centred * lax.rsqrt(spread + EPS)

    cond_norm = norm(cond_ref[...]).astype(BF16)
    normed = [norm(atoms_ref[s, pl.ds(0, atoms)]) for s in range(samples)]
    for which in range(2):
        adapt = mm(cond_norm, ada_ref[which])
        mod_ref[3 * which, pl.ds(0, atoms)] = jax.nn.sigmoid(
            adapt[:, :width] + ada_bias_ref[which : which + 1]
        )
        mod_ref[3 * which + 1, pl.ds(0, atoms)] = adapt[:, width:]
    zeroed = mm(cond_norm, jnp.concatenate([zero_ref[0], zero_ref[1]], axis=1))
    for which in range(2):
        mod_ref[3 * which + 2, pl.ds(0, atoms)] = jax.nn.sigmoid(
            zeroed[:, which * width : (which + 1) * width] + zero_bias_ref[which : which + 1]
        )

    factor = head_dim**-0.5

    def as_query(projected):
        return ((projected + query_bias_ref[...]) * factor).astype(BF16)

    own = pl.ds(0, atoms)
    for s in range(samples):
        attn_in = (normed[s] * mod_ref[0, own] + mod_ref[1, own]).astype(BF16)
        projected = mm(attn_in, qkvg_ref[...])
        q_ref[s, own] = as_query(projected[:, :width])
        kv_ref[s, pl.ds(wide, atoms), pl.ds(0, 2 * width)] = projected[
            :, width : 3 * width
        ].astype(BF16)
        gate_ref[s, own] = jax.nn.sigmoid(projected[:, 3 * width :])

    weight = pair_weight_ref[...]
    weight = weight - jnp.mean(weight, axis=1, keepdims=True)
    spread_c = jnp.where(
        iota((channels, rows_half), 1) % channels == iota((channels, rows_half), 0), 1.0, 0.0
    ).astype(BF16)
    own_query = iota((half, rows_half), 1) // channels == iota((half, rows_half), 0)
    remaining = weight
    for piece in range(3):
        part = remaining.astype(BF16)
        remaining = remaining - part.astype(F32)
        broad = mm(part, spread_c)
        blocks = [
            jnp.where(own_query, jnp.broadcast_to(broad[h : h + 1], (half, rows_half)), 0.0)
            for h in range(heads)
        ]
        lhs_ref[pl.ds(rows_half + piece * lines, lines)] = jnp.concatenate(
            blocks, axis=0
        ).astype(BF16)

    def pair_window(w, block, keep):
        both = jnp.concatenate([block[:rows_half], block[rows_half:]], axis=1)
        result = mm(lhs_ref[...], both)
        square = None
        for c in range(channels):
            centred = result[c * half : (c + 1) * half]
            square = centred * centred if c == 0 else square + centred * centred
        at = rows_half
        total = (
            result[at : at + lines]
            + result[at + lines : at + 2 * lines]
            + result[at + 2 * lines : at + 3 * lines]
        )
        scale = lax.rsqrt(square * (1.0 / channels) + EPS)
        bias = total * jnp.concatenate([scale] * heads, axis=0)
        if keep is not None:
            bias = jnp.where(jnp.concatenate(keep, axis=1)[0:1] > 0.5, bias, DEAD)
        bias_ref[w, pl.ds(0, lines)] = bias[:, :key_len]
        bias_ref[w, pl.ds(lines, lines)] = bias[:, key_len:]

    def as_row(ref):
        return ref[...].reshape(1, atoms)

    def usable_at(mask, position):
        return (
            (mask == 1)
            & (position >= 0)
            & (position < n * atoms)
            & (position < count_ref[0])
        )

    def alive(usable):
        return jnp.broadcast_to(jnp.where(usable, 1.0, 0.0), (8, usable.shape[1]))

    def lanes_from(row, start, size):
        length = row.shape[1]
        return pltpu.roll(row, (length - start) % length, axis=1)[:, :size]

    inner = [
        w
        for w in range(windows)
        if w * query_len >= margin and w * query_len - margin + key_len <= atoms
    ]
    outer = [w for w in range(windows) if w not in inner]
    live = alive(usable_at(as_row(mask_ref), me * atoms + iota((1, atoms), 1)))
    for copy in pair_copies:
        copy.wait()
    for copy in loads[len(early) :]:
        copy.wait()
    sends([4])
    for w in inner:
        pair_window(w, pair_buf[w], [lanes_from(live, w * query_len - margin, key_len)] * 2)
    for w in outer:
        pair_window(w, pair_buf[w], None)

    head_of = iota((half, width), 1) // head_dim
    blank = jnp.zeros((key_len, width), BF16)

    def tiles_of(w, s):
        return [(t, (w + 1) * query_len, w * query_len, query_len, w, 0) for t in (s, s + 1)]

    def far_tiles(s):
        return [
            (s, 0, atoms, half, windows, 0),
            (s, atoms + 2 * wide - key_len, atoms + half, half, windows, lines),
        ]

    def stacked(s, row, count):
        query = q_ref[s, pl.ds(row, count)]
        parts = []
        for at in range(0, count, half):
            piece = query[at : at + half]
            for h in range(heads):
                parts.append(jnp.where(head_of == h, piece, jnp.zeros_like(piece)))
        return jnp.concatenate(parts, axis=0)

    def score(tiles):
        both = jnp.concatenate([stacked(s, row, m) for s, _, row, m, _, _ in tiles], axis=1)
        tall = []
        for s, key, _, _, _, _ in tiles:
            line = [blank] * len(tiles)
            line[len(tall)] = kv_ref[s, pl.ds(key, key_len), pl.ds(0, width)]
            tall.append(jnp.concatenate(line, axis=1))
        scores = lax.dot_general(
            both,
            jnp.concatenate(tall, axis=0),
            (((1,), (1,)), ((), ())),
            preferred_element_type=F32,
        )
        found = []
        for i, (_, _, _, m, w, line) in enumerate(tiles):
            own = scores[:, i * key_len : (i + 1) * key_len]
            own = own + bias_ref[w, pl.ds(line, heads * m)]
            found.append((own, jnp.max(own, axis=1, keepdims=True)))
        return found

    def mix(tiles, found):
        return [
            mm(
                jnp.exp(own - top).astype(BF16),
                kv_ref[s, pl.ds(key, key_len), pl.ds(width, 2 * width)],
            )
            for (s, key, _, _, _, _), (own, top) in zip(tiles, found)
        ]

    def blend(tiles, mixes):
        for (s, _, row, m, _, _), mixed in zip(tiles, mixes):
            rows = pl.ds(row, m)
            outs = []
            for base in range(0, heads * m, lines):
                value = mixed[base : base + half, :width]
                amount = mixed[base : base + half, width:]
                for h in range(1, heads):
                    at = base + h * half
                    value = jnp.where(head_of == h, mixed[at : at + half, :width], value)
                    amount = jnp.where(head_of == h, mixed[at : at + half, width:], amount)
                outs.append(value / amount)
            blend_ref[s, rows] = (jnp.concatenate(outs, axis=0) * gate_ref[s, rows]).astype(BF16)

    def transition(parts):
        def gather(ref):
            return jnp.concatenate([ref[s, pl.ds(a, m)] for s, a, m in parts], axis=0)

        def modulation(k):
            return jnp.concatenate([mod_ref[k, pl.ds(a, m)] for _, a, m in parts], axis=0)

        mixed = mm(gather(blend_ref), out_ref[...])
        yield
        after = (gather(atoms_ref).astype(F32) + modulation(2) * mixed).astype(BF16)
        trans_in = (norm(after) * modulation(3) + modulation(4)).astype(BF16)
        mixed = mm(trans_in, swiglu_ref[...])
        yield
        units = (jax.nn.silu(mixed[:, :hidden]) * mixed[:, hidden:]).astype(BF16)
        mixed = mm(units, down_ref[...])
        yield
        final = (after.astype(F32) + modulation(5) * mixed).astype(BF16)
        features = jnp.maximum(mm(final, token_weight_ref[...]), 0.0).astype(BF16)
        at = 0
        for s, a, m in parts:
            kept = min(a + m, atoms) - a
            atoms_out_ref[s, pl.ds(a, kept)] = final[at : at + kept]
            feat_ref[s, pl.ds(a, m)] = features[at : at + m]
            at += m
        yield

    def attention(units):
        found, mixes = {}, {}
        for i in range(len(units) + MIX_LAG + BLEND_LAG):
            if i < len(units):
                found[i] = score(units[i])
            j = i - MIX_LAG
            if 0 <= j < len(units):
                mixes[j] = mix(units[j], found.pop(j))
            j = j - BLEND_LAG
            if 0 <= j < len(units):
                blend(units[j], mixes.pop(j))
            yield

    def rotate(streams):
        streams = list(streams)
        while streams:
            for stream in list(streams):
                if next(stream, streams) is streams:
                    streams.remove(stream)
                else:
                    yield

    for _ in attention([tiles_of(w, s) for w in inner for s in range(0, samples, 2)]):
        pass

    for to_there, out_there, in_there in (
        (to_right, has_right, has_left),
        (to_left, has_left, has_right),
    ):

        @pl.when(out_there)
        def _(copies=to_there):
            for copy in copies:
                copy.wait_send()

        @pl.when(in_there)
        def _(copies=to_there):
            for copy in copies:
                copy.wait_recv()

    extent = atoms + 2 * lanes

    def extended(halo, ref):
        return jnp.concatenate(
            [as_row(halo[0])[:, atoms - lanes :], as_row(ref), as_row(halo[1])[:, :lanes]],
            axis=1,
        )

    usable = usable_at(extended(halo_m, mask_ref), me * atoms - lanes + iota((1, extent), 1))
    relative = jnp.where(usable, extended(halo_t, token_ref) - me * tokens, -2)
    live = alive(usable)

    def halo():
        near = [pl.ds(wide - half, half), pl.ds(0, half)]
        for side in range(2):
            atoms_ref[:, pl.ds(atoms + side * half, half)] = halo_x[side, :, near[side]]
        cond_norm = norm(jnp.concatenate([halo_c[0], halo_c[1]], axis=0)).astype(BF16)
        normed = norm(
            jnp.concatenate(
                [halo_x[side].reshape(samples * wide, width) for side in range(2)], axis=0
            )
        ).reshape(2, samples, wide, width)
        adapt = mm(cond_norm, ada_ref[0])
        close = jnp.concatenate([cond_norm[wide - half : wide], cond_norm[wide : wide + half]], axis=0)
        close_adapt = mm(close, ada_ref[1])
        zeroed = mm(close, jnp.concatenate([zero_ref[0], zero_ref[1]], axis=1))
        far = [
            lanes_from(live, lanes - wide, key_len),
            lanes_from(live, lanes + atoms + wide - key_len, key_len),
        ]
        pair_window(windows, pair_far[...], far)
        yield
        for w in outer:
            keep = lanes_from(live, lanes + w * query_len - margin, key_len)[0:1] > 0.5
            bias_ref[w] = jnp.where(keep, bias_ref[w], DEAD)
        extra = pl.ds(atoms, 2 * half)
        mod_ref[3, extra] = jax.nn.sigmoid(close_adapt[:, :width] + ada_bias_ref[1:2])
        mod_ref[4, extra] = close_adapt[:, width:]
        for which in range(2):
            mod_ref[3 * which + 2, extra] = jax.nn.sigmoid(
                zeroed[:, which * width : (which + 1) * width] + zero_bias_ref[which : which + 1]
            )
        scale = jax.nn.sigmoid(adapt[:, :width] + ada_bias_ref[0:1])
        attn_in = (
            normed * scale.reshape(2, 1, wide, width)
            + adapt[:, width:].reshape(2, 1, wide, width)
        ).astype(BF16)
        projected = mm(
            attn_in.reshape(2 * samples * wide, width), qkvg_ref[:, pl.ds(width, 2 * width)]
        )
        close = jnp.concatenate(
            [
                attn_in[side, s, at : at + half]
                for s in range(samples)
                for side, at in enumerate((wide - half, 0))
            ],
            axis=0,
        )
        sides = mm(
            close,
            jnp.concatenate(
                [qkvg_ref[:, pl.ds(0, width)], qkvg_ref[:, pl.ds(3 * width, width)]], axis=1
            ),
        ).reshape(samples, 2 * half, 2 * width)
        yield
        for side, there in enumerate((has_left, has_right)):
            own = projected[side * samples * wide : (side + 1) * samples * wide]
            own = jnp.where(there, own, 0.0).astype(BF16)
            start = side * (wide + atoms)
            kv_ref[:, pl.ds(start, wide), pl.ds(0, 2 * width)] = own.reshape(
                samples, wide, 2 * width
            )
        for s in range(samples):
            q_ref[s, extra] = as_query(sides[s, :, :width])
            gate_ref[s, extra] = jax.nn.sigmoid(sides[s, :, width:])
        yield

    first, count = inner[0] * query_len, len(inner) * query_len
    fill = rotate([transition([(s, first, count)]) for s in range(samples)])
    for _ in halo():
        for _ in range(FILL_HALO):
            next(fill, None)
    units = [tiles_of(w, s) for w in outer for s in range(0, samples, 2)]
    units += [far_tiles(s) for s in range(samples)]
    for i, _ in enumerate(attention(units)):
        if i % FILL_EVERY == 0:
            next(fill, None)

    strip = iota((1, extent), 1)
    beyond = jnp.where(
        strip < half,
        pltpu.roll(jnp.broadcast_to(relative, (8, extent)), extent - lanes + half, axis=1)[0:1],
        pltpu.roll(jnp.broadcast_to(relative, (8, extent)), extent - lanes - atoms + half, axis=1)[0:1],
    )[:, : 2 * half]
    chosen = jnp.concatenate([relative[:, lanes : lanes + atoms], beyond], axis=1)
    total_atoms = atoms + 2 * half
    hits = iota((tokens, extent), 0) == jnp.broadcast_to(relative, (tokens, extent))
    per_count = 1.0 / jnp.maximum(
        jnp.sum(jnp.where(hits, 1.0, 0.0), axis=1, keepdims=True), 1.0
    )
    onehot = jnp.where(
        iota((tokens, total_atoms), 0) == jnp.broadcast_to(chosen, (tokens, total_atoms)), 1.0, 0.0
    ).astype(BF16)

    def closing(s):
        yield from transition(
            [(s, 0, first), (s, first + count, atoms - first - count + 2 * half)]
        )
        tokens_out_ref[s] = (mm(onehot, feat_ref[s]) * per_count).astype(BF16)
        yield

    for _ in rotate([fill] + [closing(s) for s in range(samples)]):
        pass


def on_device(
    n,
    atoms_in, cond, pair, atom_mask, atom_count, atom_to_token, ada_weight, ada_bias,
    zero_weight, zero_bias, qkvg_weight, query_bias, pair_weight, out_weight,
    swiglu_weight, down_weight, token_weight,
):
    samples, atoms, width = atoms_in.shape
    windows, query_len, channels, key_len = pair.shape
    heads = pair_weight.shape[0]
    wide = (key_len + query_len) // 2
    spread = atoms + query_len
    tokens = atoms // ATOMS_PER_TOKEN
    token_width = token_weight.shape[1]
    half = query_len // 2
    rows_half = half * channels
    vmem = pl.BlockSpec(memory_space=pltpu.VMEM)
    hbm = pl.BlockSpec(memory_space=pltpu.HBM)
    query_bias = query_bias.reshape(1, width)
    staged = (
        cond, ada_weight, ada_bias, zero_weight, zero_bias, qkvg_weight,
        query_bias, pair_weight, out_weight, swiglu_weight, down_weight, token_weight,
        atom_mask, atom_to_token,
    )
    return pl.pallas_call(
        functools.partial(block_body, n),
        out_shape=(
            pltpu.VMEM(atoms_in.shape, BF16),
            pltpu.VMEM((samples, tokens, token_width), BF16),
        ),
        in_specs=[hbm] * 17,
        out_specs=(vmem, vmem),
        scratch_shapes=[pltpu.VMEM(a.shape, a.dtype) for a in staged]
        + [
            pltpu.SMEM(atom_count.shape, atom_count.dtype),
            pltpu.VMEM((samples, spread, width), BF16),
            pltpu.VMEM((windows, query_len * channels, key_len), BF16),
            pltpu.VMEM((query_len * channels, key_len), BF16),
            pltpu.VMEM((2, samples, wide, width), BF16),
            pltpu.VMEM((2, wide, width), BF16),
            pltpu.VMEM((atoms,), jnp.int32),
            pltpu.VMEM((atoms,), jnp.int32),
            pltpu.VMEM((atoms,), jnp.int32),
            pltpu.VMEM((atoms,), jnp.int32),
            pltpu.VMEM((samples, atoms + 2 * wide, 3 * width), BF16),
            pltpu.VMEM((samples, spread, width), BF16),
            pltpu.VMEM((samples, spread, width), F32),
            pltpu.VMEM((windows + 1, heads * query_len, key_len), F32),
            pltpu.VMEM((6, spread, width), F32),
            pltpu.VMEM((samples, spread, token_width), BF16),
            pltpu.VMEM((samples, spread, width), BF16),
            pltpu.VMEM((rows_half + 3 * heads * half, rows_half), BF16),
            pltpu.SemaphoreType.DMA((len(staged) + 2,)),
            pltpu.SemaphoreType.DMA((1,)),
            pltpu.SemaphoreType.DMA((2, 5)),
            pltpu.SemaphoreType.DMA((2, 5)),
        ],
        compiler_params=pltpu.CompilerParams(collective_id=0, has_side_effects=True),
        name="atom_block",
    )(
        atoms_in, cond, pair.reshape(windows, query_len * channels, key_len),
        atom_mask, atom_to_token, atom_count,
        ada_weight, ada_bias, zero_weight, zero_bias, qkvg_weight,
        query_bias, pair_weight, out_weight, swiglu_weight,
        down_weight, token_weight,
    )


def solution(mesh):
    shard = P(("struct", "atom"))
    stream = P("struct", "atom", None)
    in_specs = (stream, shard, shard, shard, P("struct"), shard) + (P(),) * 11
    return jax.shard_map(
        functools.partial(on_device, mesh.shape["atom"]),
        mesh=mesh,
        in_specs=in_specs,
        out_specs=(stream, stream),
        check_vma=False,
    )
```

time: 14.9 us -> 14.5 us (0.973)
  Pallas kernels: 11.9 us -> 11.6 us
    pallas_call x1, Pallas kernels: 11.9 us -> 11.6 us  [on_device(): pl.pallas_call(functools.partial(block_body, n), out_shape=(pltpu.VMEM(at...]
where the time goes in v2:
time: 14.5 us; the launch traced here: 14.4 us
  Pallas kernels  11.6 us (80%)
  local copies, waits for them, and re-layouts  1.46 us (10%)
  between operations  1.29 us (9%)
    pallas_call x1, Pallas kernels, on_device(): pl.pallas_call(functools.partial(block_body, n), out_shape=(pltpu.VMEM(at...  11.6 us
    unnamed x2, local copies, waits for them, and re-layouts  1.46 us

profile of v2, /device:TPU:1, one launch (start us, length us, event | category | flops | bytes accessed | tf_op | source)
XLA Modules:
  0.0 14.4 jit_solution(4109459270605272028)
XLA Ops:
  1.3 11.6 %atom_block.1 = (bf16[4,384,128]{2,1,0:T(8,128)(2,1)S(1)}, bf16[4,48,768]{2,1,0:T(8,128)(2,1)S(1)}) custom-call(bf16[4,384,128]{2,1,0:T(8,128)(2,1)} %atoms_hbm.1, bf16[384,128]{1,0:T(8,128)(2,1)} %cond_hbm.1, bf16[12,512,128]{2,1,0:T(8,128)(2,1)} %bitcast.2, s32[384]{0:T(512)} %mask_hbm.1, s32[384]{0:T(512)} %token_hbm.1, s32[1]{0:T(128)S(6)} %copy.23.count_hbm, ...), custom_call_target="tpu_custom_call" | custom-call | tf_op jit(solution)/shard_map/atom_block/pallas_call | solution.py:542
  12.9 0.7 %copy.21 = bf16[4,384,128]{2,1,0:T(8,128)(2,1)} copy(bf16[4,384,128]{2,1,0:T(8,128)(2,1)S(1)} %get-tuple-element.2) | data formatting | bytes 786432
  13.7 0.7 %copy.22 = bf16[4,48,768]{2,1,0:T(8,128)(2,1)} copy(bf16[4,48,768]{2,1,0:T(8,128)(2,1)S(1)} %get-tuple-element.3) | data formatting | bytes 589824

commit v3 on v2

--- a/solution.py
+++ b/solution.py
@@ -10,8 +10,9 @@
 ATOMS_PER_TOKEN = 8
 EPS = 1e-05
 DEAD = -1e30
-MIX_LAG = 2
+MIX_LAG = 4
 BLEND_LAG = 1
+AHEAD = 8
 FILL_HALO = 2
 FILL_EVERY = 2
 MESH = pl.DeviceIdType.MESH
@@ -38,7 +39,7 @@
     mask_ref, token_ref, count_ref, atoms_ref,
     pair_buf, pair_far, halo_x, halo_c, halo_m0, halo_m1, halo_t0, halo_t1,
     kv_ref, q_ref, gate_ref, bias_ref, mod_ref, feat_ref, blend_ref, lhs_ref,
-    load_sem, pair_sem, send_sem, recv_sem,
+    load_sem, pair_sem, send_sem, recv_sem, ready_sem,
 ):
     samples, atoms, width = atoms_out_ref.shape
     windows, rows_pair, key_len = pair_ref.shape
@@ -62,21 +63,17 @@
     barrier = pltpu.get_barrier_semaphore()
     has_left, has_right = me > 0, me < n - 1
 
-    @pl.when(has_left)
-    def _():
-        pl.semaphore_signal(barrier, inc=1, device_id={"atom": left}, device_id_type=MESH)
-
     @pl.when(has_right)
     def _():
         pl.semaphore_signal(barrier, inc=1, device_id={"atom": right}, device_id_type=MESH)
 
 
+    pair_copy = pltpu.make_async_copy(pair_ref, pair_buf, pair_sem.at[0])
     early = (
         (cond_hbm, cond_ref), (atoms_hbm, atoms_ref.at[:, pl.ds(0, atoms)]), (ada_hbm, ada_ref),
         (ada_bias_hbm, ada_bias_ref), (zero_hbm, zero_ref), (zero_bias_hbm, zero_bias_ref),
-        (qkvg_hbm, qkvg_ref), (query_bias_hbm, query_bias_ref),
-        (pair_weight_hbm, pair_weight_ref), (mask_hbm, mask_ref), (token_hbm, token_ref),
-        (count_hbm, count_ref),
+        (qkvg_hbm, qkvg_ref), (query_bias_hbm, query_bias_ref), (mask_hbm, mask_ref),
+        (token_hbm, token_ref), (pair_weight_hbm, pair_weight_ref), (count_hbm, count_ref),
     )
     late = (
         (out_hbm, out_ref), (swiglu_hbm, swiglu_ref), (down_hbm, down_ref),
@@ -88,8 +85,7 @@
     ]
     for copy in loads[: len(early)]:
         copy.start()
-    pair_copies = [pltpu.make_async_copy(pair_ref, pair_buf, pair_sem.at[0])]
-    pair_copies[0].start()
+    pair_copy.start()
     for copy in loads[len(early) :]:
         copy.start()
 
@@ -127,7 +123,7 @@
                 (mask_ref, halo_m[side]),
                 (token_ref, halo_t[side]),
                 (
-                    pair_buf.at[far[0], pl.ds(far[1], size)],
+                    pair_ref.at[far[0], pl.ds(far[1], size)],
                     pair_far.at[pl.ds(skipped + side * size, size)],
                 ),
             )
@@ -144,58 +140,70 @@
             )
     to_right, to_left = copies[:5], copies[5:]
 
-    def sends(chosen):
-        @pl.when(has_right)
-        def _():
-            for k in chosen:
-                to_right[k].start()
-
-        @pl.when(has_left)
-        def _():
-            for k in chosen:
-                to_left[k].start()
-
-    for copy in loads[: len(early)]:
-        copy.wait()
-
-    pl.semaphore_wait(barrier, (me + n - 1) // n + (2 * n - 2 - me) // n)
-
-    sends(range(4))
-
     def norm(values):
         values = values.astype(F32)
         centred = values - jnp.sum(values, axis=1, keepdims=True) * inverse
         spread = jnp.sum(centred * centred, axis=1, keepdims=True) * inverse
         return centred * lax.rsqrt(spread + EPS)
 
-    cond_norm = norm(cond_ref[...]).astype(BF16)
-    normed = [norm(atoms_ref[s, pl.ds(0, atoms)]) for s in range(samples)]
-    for which in range(2):
-        adapt = mm(cond_norm, ada_ref[which])
-        mod_ref[3 * which, pl.ds(0, atoms)] = jax.nn.sigmoid(
-            adapt[:, :width] + ada_bias_ref[which : which + 1]
-        )
-        mod_ref[3 * which + 1, pl.ds(0, atoms)] = adapt[:, width:]
-    zeroed = mm(cond_norm, jnp.concatenate([zero_ref[0], zero_ref[1]], axis=1))
-    for which in range(2):
-        mod_ref[3 * which + 2, pl.ds(0, atoms)] = jax.nn.sigmoid(
-            zeroed[:, which * width : (which + 1) * width] + zero_bias_ref[which : which + 1]
-        )
-
+    @pl.when(has_left)
+    def _():
+        pl.semaphore_wait(barrier, 1)
+        pl.semaphore_signal(ready_sem, inc=1, device_id={"atom": left}, device_id_type=MESH)
+
+    for copy in loads[: len(early)]:
+        copy.wait()
+
+    @pl.when(has_left)
+    def _():
+        for copy in to_left:
+            copy.start()
+
+    own = pl.ds(0, atoms)
     factor = head_dim**-0.5
 
     def as_query(projected):
         return ((projected + query_bias_ref[...]) * factor).astype(BF16)
 
-    own = pl.ds(0, atoms)
-    for s in range(samples):
-        attn_in = (normed[s] * mod_ref[0, own] + mod_ref[1, own]).astype(BF16)
+    def conditioning():
+        cond_norm = norm(cond_ref[...]).astype(BF16)
+        yield
+        for which in range(2):
+            adapt = mm(cond_norm, ada_ref[which])
+            mod_ref[3 * which, own] = jax.nn.sigmoid(
+                adapt[:, :width] + ada_bias_ref[which : which + 1]
+            )
+            mod_ref[3 * which + 1, own] = adapt[:, width:]
+            yield
+        zeroed = mm(cond_norm, jnp.concatenate([zero_ref[0], zero_ref[1]], axis=1))
+        for which in range(2):
+            mod_ref[3 * which + 2, own] = jax.nn.sigmoid(
+                zeroed[:, which * width : (which + 1) * width] + zero_bias_ref[which : which + 1]
+            )
+        yield
+
+    def projection(s):
+        normed = norm(atoms_ref[s, own])
+        yield
+        attn_in = (normed * mod_ref[0, own] + mod_ref[1, own]).astype(BF16)
         projected = mm(attn_in, qkvg_ref[...])
         q_ref[s, own] = as_query(projected[:, :width])
         kv_ref[s, pl.ds(wide, atoms), pl.ds(0, 2 * width)] = projected[
             :, width : 3 * width
         ].astype(BF16)
         gate_ref[s, own] = jax.nn.sigmoid(projected[:, 3 * width :])
+        yield
+
+    starts = [conditioning(), projection(0), projection(1)]
+    for stream in starts:
+        next(stream)
+    for stream in starts:
+        for _ in stream:
+            pass
+
+    for copy in loads[len(early) :]:
+        copy.wait()
+    pair_copy.wait()
 
     weight = pair_weight_ref[...]
     weight = weight - jnp.mean(weight, axis=1, keepdims=True)
@@ -261,15 +269,14 @@
     ]
     outer = [w for w in range(windows) if w not in inner]
     live = alive(usable_at(as_row(mask_ref), me * atoms + iota((1, atoms), 1)))
-    for copy in pair_copies:
-        copy.wait()
-    for copy in loads[len(early) :]:
-        copy.wait()
-    sends([4])
-    for w in inner:
-        pair_window(w, pair_buf[w], [lanes_from(live, w * query_len - margin, key_len)] * 2)
-    for w in outer:
-        pair_window(w, pair_buf[w], None)
+    def pairs():
+        for w in inner:
+            keep = lanes_from(live, w * query_len - margin, key_len)
+            pair_window(w, pair_buf[w], [keep, keep])
+            yield
+        for w in outer:
+            pair_window(w, pair_buf[w], None)
+            yield
 
     head_of = iota((half, width), 1) // head_dim
     blank = jnp.zeros((key_len, width), BF16)
@@ -383,8 +390,34 @@
                 else:
                     yield
 
-    for _ in attention([tiles_of(w, s) for w in inner for s in range(0, samples, 2)]):
-        pass
+    def series(*streams):
+        for stream in streams:
+            yield from stream
+
+    def together(main, side, start, every):
+        for i, _ in enumerate(main):
+            if i >= start and (i - start) % every == 0:
+                next(side, None)
+
+    first, count = inner[0] * query_len, len(inner) * query_len
+    bias_steps = pairs()
+    together(bias_steps, series(projection(2), projection(3)), 1, 2)
+
+    @pl.when(has_right)
+    def _():
+        pl.semaphore_wait(ready_sem, 1)
+        for copy in to_right:
+            copy.start()
+
+    units = [tiles_of(w, s) for s in range(0, samples, 2) for w in inner]
+    lag = MIX_LAG + BLEND_LAG
+    fill = rotate([transition([(s, first, count)]) for s in range(2)])
+    for i, _ in enumerate(attention(units)):
+        if i >= len(inner) + lag:
+            next(fill, None)
+    fill = series(fill, rotate([transition([(s, first, count)]) for s in range(2, samples)]))
+    for _ in range(AHEAD):
+        next(fill, None)
 
     for to_there, out_there, in_there in (
         (to_right, has_right, has_left),
@@ -478,17 +511,6 @@
             gate_ref[s, extra] = jax.nn.sigmoid(sides[s, :, width:])
         yield
 
-    first, count = inner[0] * query_len, len(inner) * query_len
-    fill = rotate([transition([(s, first, count)]) for s in range(samples)])
-    for _ in halo():
-        for _ in range(FILL_HALO):
-            next(fill, None)
-    units = [tiles_of(w, s) for w in outer for s in range(0, samples, 2)]
-    units += [far_tiles(s) for s in range(samples)]
-    for i, _ in enumerate(attention(units)):
-        if i % FILL_EVERY == 0:
-            next(fill, None)
-
     strip = iota((1, extent), 1)
     beyond = jnp.where(
         strip < half,
@@ -512,7 +534,20 @@
         tokens_out_ref[s] = (mm(onehot, feat_ref[s]) * per_count).astype(BF16)
         yield
 
-    for _ in rotate([fill] + [closing(s) for s in range(samples)]):
+    for _ in halo():
+        for _ in range(FILL_HALO):
+            next(fill, None)
+    units = []
+    for s in range(0, samples, 2):
+        units += [tiles_of(w, s) for w in outer] + [far_tiles(s), far_tiles(s + 1)]
+    ready = len(units) // 2 + MIX_LAG + BLEND_LAG
+    begun = rotate([closing(s) for s in range(samples // 2)])
+    for i, _ in enumerate(attention(units)):
+        if i >= ready:
+            next(begun, None)
+        elif i % FILL_EVERY == 0:
+            next(fill, None)
+    for _ in rotate([begun, fill] + [closing(s) for s in range(samples // 2, samples)]):
         pass
 
 
@@ -571,6 +606,7 @@
             pltpu.SemaphoreType.DMA((1,)),
             pltpu.SemaphoreType.DMA((2, 5)),
             pltpu.SemaphoreType.DMA((2, 5)),
+            pltpu.SemaphoreType.REGULAR,
         ],
         compiler_params=pltpu.CompilerParams(collective_id=0, has_side_effects=True),
         name="atom_block",

time: 14.5 us -> 13 us (0.90)
  Pallas kernels: 11.6 us -> 10.1 us
    pallas_call x1, Pallas kernels: 11.6 us -> 10.1 us  [on_device(): pl.pallas_call(functools.partial(block_body, n), out_shape=(pltpu.VMEM(at...]
where the time goes in v3:
time: 13 us; the launch traced here: 12.8 us
  Pallas kernels  10.1 us (78%)
  local copies, waits for them, and re-layouts  1.46 us (11%)
  between operations  1.29 us (10%)
    pallas_call x1, Pallas kernels, on_device(): pl.pallas_call(functools.partial(block_body, n), out_shape=(pltpu.VMEM(at...  10.1 us
    unnamed x2, local copies, waits for them, and re-layouts  1.46 us

profile of v3, /device:TPU:1, one launch (start us, length us, event | category | flops | bytes accessed | tf_op | source)
XLA Modules:
  0.0 12.8 jit_solution(8351738307772405349)
XLA Ops:
  1.3 10.1 %atom_block.1 = (bf16[4,384,128]{2,1,0:T(8,128)(2,1)S(1)}, bf16[4,48,768]{2,1,0:T(8,128)(2,1)S(1)}) custom-call(bf16[4,384,128]{2,1,0:T(8,128)(2,1)} %atoms_hbm.1, bf16[384,128]{1,0:T(8,128)(2,1)} %cond_hbm.1, bf16[12,512,128]{2,1,0:T(8,128)(2,1)} %bitcast.2, s32[384]{0:T(512)} %mask_hbm.1, s32[384]{0:T(512)} %token_hbm.1, s32[1]{0:T(128)S(6)} %copy.23.count_hbm, ...), custom_call_target="tpu_custom_call" | custom-call | tf_op jit(solution)/shard_map/atom_block/pallas_call | solution.py:577
  11.4 0.7 %copy.21 = bf16[4,384,128]{2,1,0:T(8,128)(2,1)} copy(bf16[4,384,128]{2,1,0:T(8,128)(2,1)S(1)} %get-tuple-element.2) | data formatting | bytes 786432
  12.1 0.7 %copy.22 = bf16[4,48,768]{2,1,0:T(8,128)(2,1)} copy(bf16[4,48,768]{2,1,0:T(8,128)(2,1)S(1)} %get-tuple-element.3) | data formatting | bytes 589824

commit v4 on v3

--- a/solution.py
+++ b/solution.py
@@ -12,8 +12,9 @@
 DEAD = -1e30
 MIX_LAG = 4
 BLEND_LAG = 1
-AHEAD = 8
-FILL_HALO = 2
+AHEAD = 0
+T_LATE = 2
+FILL_HALO = 3
 FILL_EVERY = 2
 MESH = pl.DeviceIdType.MESH
 F32 = jnp.float32
@@ -30,15 +31,15 @@
 
 def block_body(
     n,
-    atoms_hbm, cond_hbm, pair_ref, mask_hbm, token_hbm, count_hbm,
+    atoms_hbm, cond_hbm, pair_ref, mask_hbm, token_hbm, count_ref,
     ada_hbm, ada_bias_hbm, zero_hbm, zero_bias_hbm, qkvg_hbm, query_bias_hbm,
     pair_weight_hbm, out_hbm, swiglu_hbm, down_hbm, token_weight_hbm,
     atoms_out_ref, tokens_out_ref,
     cond_ref, ada_ref, ada_bias_ref, zero_ref, zero_bias_ref, qkvg_ref,
     query_bias_ref, pair_weight_ref, out_ref, swiglu_ref, down_ref, token_weight_ref,
-    mask_ref, token_ref, count_ref, atoms_ref,
+    mask_ref, token_ref, atoms_ref,
     pair_buf, pair_far, halo_x, halo_c, halo_m0, halo_m1, halo_t0, halo_t1,
-    kv_ref, q_ref, gate_ref, bias_ref, mod_ref, feat_ref, blend_ref, lhs_ref,
+    keys_ref, values_ref, q_ref, gate_ref, bias_ref, mod_ref, feat_ref, blend_ref, lhs_ref,
     load_sem, pair_sem, send_sem, recv_sem, ready_sem,
 ):
     samples, atoms, width = atoms_out_ref.shape
@@ -70,10 +71,11 @@
 
     pair_copy = pltpu.make_async_copy(pair_ref, pair_buf, pair_sem.at[0])
     early = (
-        (cond_hbm, cond_ref), (atoms_hbm, atoms_ref.at[:, pl.ds(0, atoms)]), (ada_hbm, ada_ref),
+        (atoms_hbm, atoms_ref.at[:, pl.ds(0, atoms)]), (cond_hbm, cond_ref),
+        (mask_hbm, mask_ref), (token_hbm, token_ref), (ada_hbm, ada_ref),
         (ada_bias_hbm, ada_bias_ref), (zero_hbm, zero_ref), (zero_bias_hbm, zero_bias_ref),
-        (qkvg_hbm, qkvg_ref), (query_bias_hbm, query_bias_ref), (mask_hbm, mask_ref),
-        (token_hbm, token_ref), (pair_weight_hbm, pair_weight_ref), (count_hbm, count_ref),
+        (qkvg_hbm, qkvg_ref), (query_bias_hbm, query_bias_ref),
+        (pair_weight_hbm, pair_weight_ref),
     )
     late = (
         (out_hbm, out_ref), (swiglu_hbm, swiglu_ref), (down_hbm, down_ref),
@@ -90,7 +92,7 @@
         copy.start()
 
     inverse = 1.0 / width
-    kv_ref[:, :, 2 * width :] = jnp.ones((samples, atoms + 2 * wide, width), BF16)
+    values_ref[:, :, width:] = jnp.ones((samples, atoms + 2 * key_len, width), BF16)
     row, col = iota((rows_half, rows_half), 0), iota((rows_half, rows_half), 1)
     place = (row % half) * channels + row // half
     same = jnp.where(row % half == col // channels, 1.0 / channels, 0.0)
@@ -151,13 +153,16 @@
         pl.semaphore_wait(barrier, 1)
         pl.semaphore_signal(ready_sem, inc=1, device_id={"atom": left}, device_id_type=MESH)
 
-    for copy in loads[: len(early)]:
+    for copy in loads[:4]:
         copy.wait()
 
     @pl.when(has_left)
     def _():
         for copy in to_left:
             copy.start()
+
+    for copy in loads[4 : len(early)]:
+        copy.wait()
 
     own = pl.ds(0, atoms)
     factor = head_dim**-0.5
@@ -188,8 +193,11 @@
         attn_in = (normed * mod_ref[0, own] + mod_ref[1, own]).astype(BF16)
         projected = mm(attn_in, qkvg_ref[...])
         q_ref[s, own] = as_query(projected[:, :width])
-        kv_ref[s, pl.ds(wide, atoms), pl.ds(0, 2 * width)] = projected[
-            :, width : 3 * width
+        key = projected[:, width : 2 * width].astype(BF16)
+        for t in range(atoms // key_len):
+            keys_ref[s, t + 1] = key[t * key_len : (t + 1) * key_len].T
+        values_ref[s, pl.ds(key_len, atoms), pl.ds(0, width)] = projected[
+            :, 2 * width : 3 * width
         ].astype(BF16)
         gate_ref[s, own] = jax.nn.sigmoid(projected[:, 3 * width :])
         yield
@@ -200,6 +208,12 @@
     for stream in starts:
         for _ in stream:
             pass
+
+    @pl.when(has_right)
+    def _():
+        pl.semaphore_wait(ready_sem, 1)
+        for copy in to_right:
+            copy.start()
 
     for copy in loads[len(early) :]:
         copy.wait()
@@ -224,7 +238,11 @@
             blocks, axis=0
         ).astype(BF16)
 
-    def pair_window(w, block, keep):
+    def turned(bias, start):
+        turn = start % key_len
+        return pltpu.roll(bias, turn, axis=1) if turn else bias
+
+    def pair_window(w, block, keep, starts):
         both = jnp.concatenate([block[:rows_half], block[rows_half:]], axis=1)
         result = mm(lhs_ref[...], both)
         square = None
@@ -241,8 +259,8 @@
         bias = total * jnp.concatenate([scale] * heads, axis=0)
         if keep is not None:
             bias = jnp.where(jnp.concatenate(keep, axis=1)[0:1] > 0.5, bias, DEAD)
-        bias_ref[w, pl.ds(0, lines)] = bias[:, :key_len]
-        bias_ref[w, pl.ds(lines, lines)] = bias[:, key_len:]
+        bias_ref[w, pl.ds(0, lines)] = turned(bias[:, :key_len], starts[0])
+        bias_ref[w, pl.ds(lines, lines)] = turned(bias[:, key_len:], starts[1])
 
     def as_row(ref):
         return ref[...].reshape(1, atoms)
@@ -269,25 +287,31 @@
     ]
     outer = [w for w in range(windows) if w not in inner]
     live = alive(usable_at(as_row(mask_ref), me * atoms + iota((1, atoms), 1)))
+    def first_key(w):
+        return key_len + w * query_len - margin
+
+    far_keys = (key_len - wide, key_len + atoms + wide - key_len)
+
     def pairs():
         for w in inner:
             keep = lanes_from(live, w * query_len - margin, key_len)
-            pair_window(w, pair_buf[w], [keep, keep])
+            pair_window(w, pair_buf[w], [keep, keep], [first_key(w)] * 2)
             yield
         for w in outer:
-            pair_window(w, pair_buf[w], None)
+            pair_window(w, pair_buf[w], None, [first_key(w)] * 2)
             yield
 
     head_of = iota((half, width), 1) // head_dim
-    blank = jnp.zeros((key_len, width), BF16)
+    blank = jnp.zeros((width, key_len), BF16)
+    lane = iota((width, key_len), 1)
 
     def tiles_of(w, s):
-        return [(t, (w + 1) * query_len, w * query_len, query_len, w, 0) for t in (s, s + 1)]
+        return [(t, first_key(w), w * query_len, query_len, w, 0) for t in (s, s + 1)]
 
     def far_tiles(s):
         return [
-            (s, 0, atoms, half, windows, 0),
-            (s, atoms + 2 * wide - key_len, atoms + half, half, windows, lines),
+            (s, far_keys[0], atoms, half, windows, 0),
+            (s, far_keys[1], atoms + half, half, windows, lines),
         ]
 
     def stacked(s, row, count):
@@ -304,14 +328,10 @@
         tall = []
         for s, key, _, _, _, _ in tiles:
             line = [blank] * len(tiles)
-            line[len(tall)] = kv_ref[s, pl.ds(key, key_len), pl.ds(0, width)]
+            t, turn = key // key_len, key % key_len
+            line[len(tall)] = jnp.where(lane < turn, keys_ref[s, t + 1], keys_ref[s, t])
             tall.append(jnp.concatenate(line, axis=1))
-        scores = lax.dot_general(
-            both,
-            jnp.concatenate(tall, axis=0),
-            (((1,), (1,)), ((), ())),
-            preferred_element_type=F32,
-        )
+        scores = mm(both, jnp.concatenate(tall, axis=0))
         found = []
         for i, (_, _, _, m, w, line) in enumerate(tiles):
             own = scores[:, i * key_len : (i + 1) * key_len]
@@ -320,13 +340,15 @@
         return found
 
     def mix(tiles, found):
-        return [
-            mm(
-                jnp.exp(own - top).astype(BF16),
-                kv_ref[s, pl.ds(key, key_len), pl.ds(width, 2 * width)],
-            )
-            for (s, key, _, _, _, _), (own, top) in zip(tiles, found)
-        ]
+        mixes = []
+        for (s, key, _, _, _, _), (own, top) in zip(tiles, found):
+            turn = key % key_len
+            split = key + key_len - turn
+            value = values_ref[s, pl.ds(key, key_len - turn)]
+            if turn:
+                value = jnp.concatenate([values_ref[s, pl.ds(split, turn)], value], axis=0)
+            mixes.append(mm(jnp.exp(own - top).astype(BF16), value))
+        return mixes
 
     def blend(tiles, mixes):
         for (s, _, row, m, _, _), mixed in zip(tiles, mixes):
@@ -403,17 +425,11 @@
     bias_steps = pairs()
     together(bias_steps, series(projection(2), projection(3)), 1, 2)
 
-    @pl.when(has_right)
-    def _():
-        pl.semaphore_wait(ready_sem, 1)
-        for copy in to_right:
-            copy.start()
-
     units = [tiles_of(w, s) for s in range(0, samples, 2) for w in inner]
     lag = MIX_LAG + BLEND_LAG
     fill = rotate([transition([(s, first, count)]) for s in range(2)])
     for i, _ in enumerate(attention(units)):
-        if i >= len(inner) + lag:
+        if i >= len(inner) + lag + T_LATE:
             next(fill, None)
     fill = series(fill, rotate([transition([(s, first, count)]) for s in range(2, samples)]))
     for _ in range(AHEAD):
@@ -464,10 +480,11 @@
             lanes_from(live, lanes - wide, key_len),
             lanes_from(live, lanes + atoms + wide - key_len, key_len),
         ]
-        pair_window(windows, pair_far[...], far)
+        pair_window(windows, pair_far[...], far, far_keys)
         yield
         for w in outer:
-            keep = lanes_from(live, lanes + w * query_len - margin, key_len)[0:1] > 0.5
+            keep = lanes_from(live, lanes + w * query_len - margin, key_len)
+            keep = turned(keep, first_key(w))[0:1] > 0.5
             bias_ref[w] = jnp.where(keep, bias_ref[w], DEAD)
         extra = pl.ds(atoms, 2 * half)
         mod_ref[3, extra] = jax.nn.sigmoid(close_adapt[:, :width] + ada_bias_ref[1:2])
@@ -501,11 +518,15 @@
         yield
         for side, there in enumerate((has_left, has_right)):
             own = projected[side * samples * wide : (side + 1) * samples * wide]
-            own = jnp.where(there, own, 0.0).astype(BF16)
-            start = side * (wide + atoms)
-            kv_ref[:, pl.ds(start, wide), pl.ds(0, 2 * width)] = own.reshape(
-                samples, wide, 2 * width
-            )
+            own = jnp.where(there, own, 0.0).astype(BF16).reshape(samples, wide, 2 * width)
+            start = key_len - wide if side == 0 else key_len + atoms
+            values_ref[:, pl.ds(start, wide), pl.ds(0, width)] = own[:, :, width:]
+            rest = jnp.zeros((key_len - wide, width), BF16)
+            for s in range(samples):
+                key = own[s, :, :width]
+                key = [rest, key] if side == 0 else [key, rest]
+                tile = 0 if side == 0 else atoms // key_len + 1
+                keys_ref[s, tile] = jnp.concatenate(key, axis=0).T
         for s in range(samples):
             q_ref[s, extra] = as_query(sides[s, :, :width])
             gate_ref[s, extra] = jax.nn.sigmoid(sides[s, :, width:])
@@ -549,6 +570,17 @@
             next(fill, None)
     for _ in rotate([begun, fill] + [closing(s) for s in range(samples // 2, samples)]):
         pass
+
+
+def flush_body(atoms_ref, tokens_ref, atoms_out_ref, tokens_out_ref, sem):
+    copies = [
+        pltpu.make_async_copy(atoms_ref, atoms_out_ref, sem.at[0]),
+        pltpu.make_async_copy(tokens_ref, tokens_out_ref, sem.at[1]),
+    ]
+    for copy in copies:
+        copy.start()
+    for copy in copies:
+        copy.wait()
 
 
 def on_device(
@@ -574,17 +606,16 @@
         query_bias, pair_weight, out_weight, swiglu_weight, down_weight, token_weight,
         atom_mask, atom_to_token,
     )
-    return pl.pallas_call(
+    held = pl.pallas_call(
         functools.partial(block_body, n),
         out_shape=(
             pltpu.VMEM(atoms_in.shape, BF16),
             pltpu.VMEM((samples, tokens, token_width), BF16),
         ),
-        in_specs=[hbm] * 17,
+        in_specs=[hbm] * 5 + [pl.BlockSpec(memory_space=pltpu.SMEM)] + [hbm] * 11,
         out_specs=(vmem, vmem),
         scratch_shapes=[pltpu.VMEM(a.shape, a.dtype) for a in staged]
         + [
-            pltpu.SMEM(atom_count.shape, atom_count.dtype),
             pltpu.VMEM((samples, spread, width), BF16),
             pltpu.VMEM((windows, query_len * channels, key_len), BF16),
             pltpu.VMEM((query_len * channels, key_len), BF16),
@@ -594,7 +625,8 @@
             pltpu.VMEM((atoms,), jnp.int32),
             pltpu.VMEM((atoms,), jnp.int32),
             pltpu.VMEM((atoms,), jnp.int32),
-            pltpu.VMEM((samples, atoms + 2 * wide, 3 * width), BF16),
+            pltpu.VMEM((samples, atoms // key_len + 2, width, key_len), BF16),
+            pltpu.VMEM((samples, atoms + 2 * key_len, 2 * width), BF16),
             pltpu.VMEM((samples, spread, width), BF16),
             pltpu.VMEM((samples, spread, width), F32),
             pltpu.VMEM((windows + 1, heads * query_len, key_len), F32),
@@ -602,7 +634,7 @@
             pltpu.VMEM((samples, spread, token_width), BF16),
             pltpu.VMEM((samples, spread, width), BF16),
             pltpu.VMEM((rows_half + 3 * heads * half, rows_half), BF16),
-            pltpu.SemaphoreType.DMA((len(staged) + 2,)),
+            pltpu.SemaphoreType.DMA((len(staged) + 1,)),
             pltpu.SemaphoreType.DMA((1,)),
             pltpu.SemaphoreType.DMA((2, 5)),
             pltpu.SemaphoreType.DMA((2, 5)),
@@ -617,6 +649,14 @@
         query_bias, pair_weight, out_weight, swiglu_weight,
         down_weight, token_weight,
     )
+    return pl.pallas_call(
+        flush_body,
+        out_shape=tuple(jax.ShapeDtypeStruct(a.shape, a.dtype) for a in held),
+        in_specs=[pl.BlockSpec(memory_space=pl.ANY)] * 2,
+        out_specs=(hbm, hbm),
+        scratch_shapes=[pltpu.SemaphoreType.DMA((2,))],
+        name="flush",
+    )(*[pltpu.with_memory_space_constraint(a, pltpu.VMEM) for a in held])
 
 
 def solution(mesh):

time: 13 us -> 12.8 us (0.985)
  local copies, waits for them, and re-layouts: 1.46 us -> 0 us
  Pallas kernels: 10.1 us -> 11.4 us
    unnamed x2 -> x0, local copies, waits for them, and re-layouts: 1.46 us -> none
    pallas_call x0 -> x1, Pallas kernels: none -> 0.86 us  [on_device(): pl.pallas_call(flush_body, out_shape=tuple((jax.ShapeDtypeStruct(a.shape,...]
    pallas_call x1, Pallas kernels: 10.1 us -> 10.5 us  [on_device(): pl.pallas_call(functools.partial(block_body, n), out_shape=(pltpu.VMEM(at...]
where the time goes in v4:
time: 12.8 us; the launch traced here: 12.7 us
  Pallas kernels  11.4 us (89%)
  between operations  1.29 us (10%)
    pallas_call x1, Pallas kernels, on_device(): pl.pallas_call(functools.partial(block_body, n), out_shape=(pltpu.VMEM(at...  10.5 us
    pallas_call x1, Pallas kernels, on_device(): pl.pallas_call(flush_body, out_shape=tuple((jax.ShapeDtypeStruct(a.shape,...  0.86 us

profile of v4, /device:TPU:1, one launch (start us, length us, event | category | flops | bytes accessed | tf_op | source)
XLA Modules:
  0.0 12.7 jit_solution(11090618560397057813)
XLA Ops:
  1.3 10.5 %atom_block.1 = (bf16[4,384,128]{2,1,0:T(8,128)(2,1)S(1)}, bf16[4,48,768]{2,1,0:T(8,128)(2,1)S(1)}) custom-call(bf16[4,384,128]{2,1,0:T(8,128)(2,1)} %atoms_hbm.1, bf16[384,128]{1,0:T(8,128)(2,1)} %cond_hbm.1, bf16[12,512,128]{2,1,0:T(8,128)(2,1)} %bitcast.2, s32[384]{0:T(512)} %mask_hbm.1, s32[384]{0:T(512)} %token_hbm.1, s32[1]{0:T(128)S(6)} %copy.19.count_ref, ...), custom_call_target="tpu_custom_call" | custom-call | tf_op jit(solution)/shard_map/atom_block/pallas_call | solution.py:609
  11.8 0.9 %flush.1 = (bf16[4,384,128]{2,1,0:T(8,128)(2,1)}, bf16[4,48,768]{2,1,0:T(8,128)(2,1)}) custom-call(bf16[4,384,128]{2,1,0:T(8,128)(2,1)S(1)} %get-tuple-element.4.atoms_ref, bf16[4,48,768]{2,1,0:T(8,128)(2,1)S(1)} %get-tuple-element.5.tokens_ref), custom_call_target="tpu_custom_call" | custom-call | tf_op jit(solution)/shard_map/flush/pallas_call | solution.py:652

commit v5 on v4

--- a/solution.py
+++ b/solution.py
@@ -12,9 +12,9 @@
 DEAD = -1e30
 MIX_LAG = 4
 BLEND_LAG = 1
-AHEAD = 0
-T_LATE = 2
-FILL_HALO = 3
+AHEAD = 4
+T_LATE = 0
+FILL_HALO = 1
 FILL_EVERY = 2
 MESH = pl.DeviceIdType.MESH
 F32 = jnp.float32
@@ -38,7 +38,7 @@
     cond_ref, ada_ref, ada_bias_ref, zero_ref, zero_bias_ref, qkvg_ref,
     query_bias_ref, pair_weight_ref, out_ref, swiglu_ref, down_ref, token_weight_ref,
     mask_ref, token_ref, atoms_ref,
-    pair_buf, pair_far, halo_x, halo_c, halo_m0, halo_m1, halo_t0, halo_t1,
+    lead_x, lead_c, pair_buf, pair_far, halo_x, halo_c, halo_m0, halo_m1, halo_t0, halo_t1,
     keys_ref, values_ref, q_ref, gate_ref, bias_ref, mod_ref, feat_ref, blend_ref, lhs_ref,
     load_sem, pair_sem, send_sem, recv_sem, ready_sem,
 ):
@@ -71,8 +71,9 @@
 
     pair_copy = pltpu.make_async_copy(pair_ref, pair_buf, pair_sem.at[0])
     early = (
-        (atoms_hbm, atoms_ref.at[:, pl.ds(0, atoms)]), (cond_hbm, cond_ref),
-        (mask_hbm, mask_ref), (token_hbm, token_ref), (ada_hbm, ada_ref),
+        (atoms_hbm.at[:, pl.ds(0, wide)], lead_x), (cond_hbm.at[pl.ds(0, wide)], lead_c),
+        (mask_hbm, mask_ref), (token_hbm, token_ref),
+        (atoms_hbm, atoms_ref.at[:, pl.ds(0, atoms)]), (cond_hbm, cond_ref), (ada_hbm, ada_ref),
         (ada_bias_hbm, ada_bias_ref), (zero_hbm, zero_ref), (zero_bias_hbm, zero_bias_ref),
         (qkvg_hbm, qkvg_ref), (query_bias_hbm, query_bias_ref),
         (pair_weight_hbm, pair_weight_ref),
@@ -120,8 +121,8 @@
         size = reach * channels
         for which, (src, dst) in enumerate(
             (
-                (atoms_ref.at[:, own], halo_x.at[side]),
-                (cond_ref.at[own], halo_c.at[side]),
+                (lead_x if side else atoms_ref.at[:, own], halo_x.at[side]),
+                (lead_c if side else cond_ref.at[own], halo_c.at[side]),
                 (mask_ref, halo_m[side]),
                 (token_ref, halo_t[side]),
                 (
@@ -205,19 +206,6 @@
     starts = [conditioning(), projection(0), projection(1)]
     for stream in starts:
         next(stream)
-    for stream in starts:
-        for _ in stream:
-            pass
-
-    @pl.when(has_right)
-    def _():
-        pl.semaphore_wait(ready_sem, 1)
-        for copy in to_right:
-            copy.start()
-
-    for copy in loads[len(early) :]:
-        copy.wait()
-    pair_copy.wait()
 
     weight = pair_weight_ref[...]
     weight = weight - jnp.mean(weight, axis=1, keepdims=True)
@@ -237,6 +225,20 @@
         lhs_ref[pl.ds(rows_half + piece * lines, lines)] = jnp.concatenate(
             blocks, axis=0
         ).astype(BF16)
+
+    for stream in starts:
+        for _ in stream:
+            pass
+
+    @pl.when(has_right)
+    def _():
+        pl.semaphore_wait(ready_sem, 1)
+        for copy in to_right:
+            copy.start()
+
+    for copy in loads[len(early) :]:
+        copy.wait()
+    pair_copy.wait()
 
     def turned(bias, start):
         turn = start % key_len
@@ -617,6 +619,8 @@
         scratch_shapes=[pltpu.VMEM(a.shape, a.dtype) for a in staged]
         + [
             pltpu.VMEM((samples, spread, width), BF16),
+            pltpu.VMEM((samples, wide, width), BF16),
+            pltpu.VMEM((wide, width), BF16),
             pltpu.VMEM((windows, query_len * channels, key_len), BF16),
             pltpu.VMEM((query_len * channels, key_len), BF16),
             pltpu.VMEM((2, samples, wide, width), BF16),
@@ -634,7 +638,7 @@
             pltpu.VMEM((samples, spread, token_width), BF16),
             pltpu.VMEM((samples, spread, width), BF16),
             pltpu.VMEM((rows_half + 3 * heads * half, rows_half), BF16),
-            pltpu.SemaphoreType.DMA((len(staged) + 1,)),
+            pltpu.SemaphoreType.DMA((len(staged) + 3,)),
             pltpu.SemaphoreType.DMA((1,)),
             pltpu.SemaphoreType.DMA((2, 5)),
             pltpu.SemaphoreType.DMA((2, 5)),

time: 12.8 us -> 12.6 us (0.984)
  Pallas kernels: 11.4 us -> 11.1 us
    pallas_call x1, Pallas kernels: 10.5 us -> 10.3 us  [on_device(): pl.pallas_call(functools.partial(block_body, n), out_shape=(pltpu.VMEM(at...]
where the time goes in v5:
time: 12.6 us; the launch traced here: 12.4 us
  Pallas kernels  11.1 us (88%)
  between operations  1.29 us (10%)
    pallas_call x1, Pallas kernels, on_device(): pl.pallas_call(functools.partial(block_body, n), out_shape=(pltpu.VMEM(at...  10.3 us
    pallas_call x1, Pallas kernels, on_device(): pl.pallas_call(flush_body, out_shape=tuple((jax.ShapeDtypeStruct(a.shape,...  0.86 us

profile of v5, /device:TPU:1, one launch (start us, length us, event | category | flops | bytes accessed | tf_op | source)
XLA Modules:
  0.0 12.4 jit_solution(3519856204651925212)
XLA Ops:
  1.3 10.3 %atom_block.1 = (bf16[4,384,128]{2,1,0:T(8,128)(2,1)S(1)}, bf16[4,48,768]{2,1,0:T(8,128)(2,1)S(1)}) custom-call(bf16[4,384,128]{2,1,0:T(8,128)(2,1)} %atoms_hbm.1, bf16[384,128]{1,0:T(8,128)(2,1)} %cond_hbm.1, bf16[12,512,128]{2,1,0:T(8,128)(2,1)} %bitcast.2, s32[384]{0:T(512)} %mask_hbm.1, s32[384]{0:T(512)} %token_hbm.1, s32[1]{0:T(128)S(6)} %copy.19.count_ref, ...), custom_call_target="tpu_custom_call" | custom-call | tf_op jit(solution)/shard_map/atom_block/pallas_call | solution.py:611
  11.6 0.9 %flush.1 = (bf16[4,384,128]{2,1,0:T(8,128)(2,1)}, bf16[4,48,768]{2,1,0:T(8,128)(2,1)}) custom-call(bf16[4,384,128]{2,1,0:T(8,128)(2,1)S(1)} %get-tuple-element.4.atoms_ref, bf16[4,48,768]{2,1,0:T(8,128)(2,1)S(1)} %get-tuple-element.5.tokens_ref), custom_call_target="tpu_custom_call" | custom-call | tf_op jit(solution)/shard_map/flush/pallas_call | solution.py:656

commit v6 on v5

--- a/solution.py
+++ b/solution.py
@@ -14,6 +14,8 @@
 BLEND_LAG = 1
 AHEAD = 4
 T_LATE = 0
+PREP_EVERY = 2
+MIX_OUT = 4
 FILL_HALO = 1
 FILL_EVERY = 2
 MESH = pl.DeviceIdType.MESH
@@ -87,9 +89,6 @@
         for i, (src, dst) in enumerate(early + late)
     ]
     for copy in loads[: len(early)]:
-        copy.start()
-    pair_copy.start()
-    for copy in loads[len(early) :]:
         copy.start()
 
     inverse = 1.0 / width
@@ -162,6 +161,9 @@
         for copy in to_left:
             copy.start()
 
+    pair_copy.start()
+    for copy in loads[len(early) :]:
+        copy.start()
     for copy in loads[4 : len(early)]:
         copy.wait()
 
@@ -226,7 +228,8 @@
             blocks, axis=0
         ).astype(BF16)
 
-    for stream in starts:
+    next(starts[0])
+    for stream in starts[1:]:
         for _ in stream:
             pass
 
@@ -392,12 +395,12 @@
             at += m
         yield
 
-    def attention(units):
+    def attention(units, ahead=MIX_LAG):
         found, mixes = {}, {}
-        for i in range(len(units) + MIX_LAG + BLEND_LAG):
+        for i in range(len(units) + ahead + BLEND_LAG):
             if i < len(units):
                 found[i] = score(units[i])
-            j = i - MIX_LAG
+            j = i - ahead
             if 0 <= j < len(units):
                 mixes[j] = mix(units[j], found.pop(j))
             j = j - BLEND_LAG
@@ -425,7 +428,9 @@
 
     first, count = inner[0] * query_len, len(inner) * query_len
     bias_steps = pairs()
-    together(bias_steps, series(projection(2), projection(3)), 1, 2)
+    together(bias_steps, series(projection(2), projection(3), starts[0]), 1, PREP_EVERY)
+    for _ in starts[0]:
+        pass
 
     units = [tiles_of(w, s) for s in range(0, samples, 2) for w in inner]
     lag = MIX_LAG + BLEND_LAG
@@ -562,10 +567,10 @@
             next(fill, None)
     units = []
     for s in range(0, samples, 2):
-        units += [tiles_of(w, s) for w in outer] + [far_tiles(s), far_tiles(s + 1)]
-    ready = len(units) // 2 + MIX_LAG + BLEND_LAG
+        units += [far_tiles(s), far_tiles(s + 1)] + [tiles_of(w, s) for w in outer]
+    ready = len(units) // 2 + MIX_OUT + BLEND_LAG
     begun = rotate([closing(s) for s in range(samples // 2)])
-    for i, _ in enumerate(attention(units)):
+    for i, _ in enumerate(attention(units, MIX_OUT)):
         if i >= ready:
             next(begun, None)
         elif i % FILL_EVERY == 0:

time: 12.6 us -> 12.5 us (level)
  no operation moved by 1% of the time
where the time goes in v6:
time: 12.5 us; the launch traced here: 12.3 us
  Pallas kernels  11 us (88%)
  between operations  1.29 us (10%)
    pallas_call x1, Pallas kernels, on_device(): pl.pallas_call(functools.partial(block_body, n), out_shape=(pltpu.VMEM(at...  10.2 us
    pallas_call x1, Pallas kernels, on_device(): pl.pallas_call(flush_body, out_shape=tuple((jax.ShapeDtypeStruct(a.shape,...  0.86 us

profile of v6, /device:TPU:1, one launch (start us, length us, event | category | flops | bytes accessed | tf_op | source)
XLA Modules:
  0.0 12.3 jit_solution(8265922435937231448)
XLA Ops:
  1.3 10.2 %atom_block.1 = (bf16[4,384,128]{2,1,0:T(8,128)(2,1)S(1)}, bf16[4,48,768]{2,1,0:T(8,128)(2,1)S(1)}) custom-call(bf16[4,384,128]{2,1,0:T(8,128)(2,1)} %atoms_hbm.1, bf16[384,128]{1,0:T(8,128)(2,1)} %cond_hbm.1, bf16[12,512,128]{2,1,0:T(8,128)(2,1)} %bitcast.2, s32[384]{0:T(512)} %mask_hbm.1, s32[384]{0:T(512)} %token_hbm.1, s32[1]{0:T(128)S(6)} %copy.19.count_ref, ...), custom_call_target="tpu_custom_call" | custom-call | tf_op jit(solution)/shard_map/atom_block/pallas_call | solution.py:616
  11.4 0.9 %flush.1 = (bf16[4,384,128]{2,1,0:T(8,128)(2,1)}, bf16[4,48,768]{2,1,0:T(8,128)(2,1)}) custom-call(bf16[4,384,128]{2,1,0:T(8,128)(2,1)S(1)} %get-tuple-element.4.atoms_ref, bf16[4,48,768]{2,1,0:T(8,128)(2,1)S(1)} %get-tuple-element.5.tokens_ref), custom_call_target="tpu_custom_call" | custom-call | tf_op jit(solution)/shard_map/flush/pallas_call | solution.py:661
